TPU v7x, 128 devices: a whole 4x4x4 slice. The times are simulated.
128 devices in a mesh: dp: 8 (over y, core), tp: 16 (over z, x).
Axes of the slice: x: 4, y: 4, z: 4, core: 2. Of those that a mesh axis runs over, the one named last changes fastest.
Arguments:
- tokens: bfloat16 [10240, 6144], P(('dp', 'tp')), parts along dimension 0, may hold values from -6 to 6
- ln_gain: float32 [6144], replicated, may hold values from 0.25 to 1.75
- ln_bias: float32 [6144], replicated, may hold values from -1.75 to 1.75
- w_qkv: bfloat16 [6144, 3, 6144], P(None, None, 'tp'), may hold values from -0.45927933 to 0.45927933
- b_qkv: float32 [3, 6144], P(None, 'tp'), may hold values from -3 to 3
- w_out: bfloat16 [6144, 6144], P('tp'), may hold values from -0.078125 to 0.078125
- b_out: float32 [6144], replicated, may hold values from -1.25 to 1.25
- kv_cache: bfloat16 [2, 96, 128, 6144], P(None, 'dp', None, 'tp'), parts along dimension 1, may hold values from -6 to 6
- page_table: int32 [8, 10], P('dp'), parts along dimension 0, may hold values from 0 to 11, as said below
- lengths: int32 [8], P('dp'), parts along dimension 0, may hold values from 641 to 1280
Outputs:
- attn_out: bfloat16 [10240, 6144], P(('dp', 'tp')), parts along dimension 0
- kv_cache_out: bfloat16 [2, 96, 128, 6144], P(None, 'dp', None, 'tp'), parts along dimension 1
There are 8 independent parts, one for each index of `dp`. A program takes and returns all parts, laid end to end along the dimension named above; an argument that names none is the same for every part. Nothing has to cross between parts.
Inputs may be any that keep to these rules, and one draw needn't show every extreme that they name: `page_table`: no slot is named twice within a part.
All inputs are finite; a program needn't handle non-finite values.
Results may differ from a plain program's by a relative error of at most 0.015.
The roundings to bfloat16 on the way count: a program that leaves them out, or rounds other values in their place, can miss the bound.
Values may be sent and summed in bfloat16 or wider, within the bound.
A program may use at most 128 MiB of HBM per device.

v0:
```python
import math

import jax
import jax.numpy as jnp
from jax import lax
from jax.sharding import PartitionSpec as P

HD = 128
SEQS = 1


norm_eps = 1e-05


def layer_norm(token_rows, gain_row, shift_row):
    floats = token_rows.astype(jnp.float32)
    center = jnp.mean(floats, axis=-1, keepdims=True)
    spread = jnp.mean(jnp.square(floats - center), axis=-1, keepdims=True)
    return ((floats - center) * lax.rsqrt(spread + norm_eps) * gain_row + shift_row).astype(
        jnp.bfloat16
    )


def attend(queries, keys, values, lengths):
    seq_count, seq_len, head_count, head_dim = queries.shape
    block_len = math.gcd(seq_len, 512)
    score_scale = 1.0 / math.sqrt(head_dim)
    key_pos = jnp.arange(seq_len, dtype=jnp.int32)

    def one_sequence(inputs):
        seq_query, seq_key, seq_value, length = inputs
        blocks = seq_query.reshape(seq_len // block_len, block_len, head_count, head_dim)

        def one_block(block_pair):
            block_query, block_index = block_pair
            scores = (
                jnp.einsum("qhe,khe->hqk", block_query, seq_key, preferred_element_type=jnp.float32)
                * score_scale
            )
            query_pos = block_index * block_len + jnp.arange(block_len, dtype=jnp.int32)
            allowed = (key_pos[None, :] <= query_pos[:, None]) & (key_pos[None, :] < length)
            scores = jnp.where(allowed[None], scores, -1e30)
            row_max = jnp.max(scores, axis=-1, keepdims=True)
            raised = jnp.exp(scores - row_max)
            weights = (raised / jnp.sum(raised, axis=-1, keepdims=True)).astype(jnp.bfloat16)
            return jnp.einsum(
                "hqk,khe->qhe", weights, seq_value, preferred_element_type=jnp.float32
            ).astype(jnp.bfloat16)

        results = lax.map(one_block, (blocks, jnp.arange(seq_len // block_len, dtype=jnp.int32)))
        return results.reshape(seq_len, head_count, head_dim)

    return lax.map(one_sequence, (queries, keys, values, lengths))


def write_cache(kv_cache, key_value, page_table, lengths):
    seq_count, page_count = page_table.shape
    page_len = kv_cache.shape[2]
    feat_here = kv_cache.shape[3]
    fresh_pages = jnp.moveaxis(key_value, 1, 0).reshape(
        2, seq_count * page_count, page_len, feat_here
    )
    slot_ids = page_table.reshape(-1)
    positions = (
        jnp.arange(page_count, dtype=jnp.int32)[:, None] * page_len
        + jnp.arange(page_len, dtype=jnp.int32)[None, :]
    )
    written = (positions[None] < lengths[:, None, None]).reshape(seq_count * page_count, page_len)
    current = kv_cache[:, slot_ids]
    new_pages = jnp.where(written[None, :, :, None], fresh_pages, current)
    return kv_cache.at[:, slot_ids].set(new_pages)


def body(tokens, ln_gain, ln_bias, w_qkv, b_qkv, w_out, b_out, kv_cache, page_table, lengths):
    model_width = tokens.shape[1]
    local_feat = w_qkv.shape[2]
    weights_flat = w_qkv.reshape(model_width, 3 * local_feat)
    bias_flat = b_qkv.reshape(-1)
    normed = layer_norm(tokens, ln_gain, ln_bias)
    block_rows = lax.all_gather(normed, "tp", axis=0, tiled=True)
    result = jnp.dot(block_rows, weights_flat, preferred_element_type=jnp.float32) + bias_flat
    projected = result.astype(jnp.bfloat16).reshape(block_rows.shape[0], 3, local_feat)
    all_rows = projected.shape[0]
    seq_len = all_rows // SEQS
    heads_here = local_feat // HD
    queries = projected[:, 0].reshape(SEQS, seq_len, heads_here, HD)
    keys = projected[:, 1].reshape(SEQS, seq_len, heads_here, HD)
    values = projected[:, 2].reshape(SEQS, seq_len, heads_here, HD)
    attended = attend(queries, keys, values, lengths).reshape(all_rows, local_feat)
    summed = lax.psum_scatter(
        jnp.dot(attended, w_out, preferred_element_type=jnp.float32).astype(jnp.bfloat16),
        "tp",
        scatter_dimension=0,
        tiled=True,
    ).astype(jnp.float32)
    attn_out = (summed + b_out).astype(jnp.bfloat16)
    kv_cache_out = write_cache(kv_cache, projected[:, 1:3], page_table, lengths)
    return (attn_out, kv_cache_out)


def solution(mesh):
    placed = (
        P(("dp", "tp"), None),
        P(),
        P(),
        P(None, None, "tp"),
        P(None, "tp"),
        P("tp", None),
        P(),
        P(None, "dp", None, "tp"),
        P("dp", None),
        P("dp"),
    )
    return jax.shard_map(
        body,
        mesh=mesh,
        in_specs=placed,
        out_specs=(P(("dp", "tp"), None), P(None, "dp", None, "tp")),
        check_vma=False,
    )
```

profile of v0, /device:TPU:0, one launch (start us, length us, event | category | flops | bytes accessed | tf_op | source)
XLA Modules:
  0.0 334.9 jit_solution(16525906927422556471)
XLA Ops:
  7.2 1.7 copy.47
  9.1 0.2 convert_reduce_fusion
  9.3 0.4 fusion.40
  9.8 1.4 fusion.43
  11.2 18.8 %copy.20 = bf16[6144,3,384]{0,2,1:T(8,128)(2,1)} copy(bf16[6144,3,384]{2,0,1:T(8,128)(2,1)} %param.15) | data formatting | bytes 28311552 | tf_op args[3]
  30.1 89.7 %all-gather.2.cloned.1.call-done = bf16[1280,6144]{1,0:T(8,128)(2,1)} async-done(((bf16[80,6144]{1,0:T(8,128)(2,1)}), bf16[1280,6144]{1,0:T(8,128)(2,1)}) %all-gather.2.cloned.1.call-update) | async-done | bytes 15728656 | tf_op jit(solution)/shard_map/all_gather | solution.py:80
  119.8 25.8 %fusion.37 = bf16[1280,1152]{0,1:T(8,128)(2,1)S(1)} fusion(bf16[1280,6144]{1,0:T(8,128)(2,1)} %all-gather.2.cloned.1.call-done, bf16[6144,1152]{0,1:T(8,128)(2,1)} %bitcast.67, f32[1152]{0:T(1024)S(1)} %add.87), kind=kOutput, calls=%fused_computation.32 | convolution fusion | flops 18122342400 | bytes 32838144 | tf_op jit(solution)/shard_map/dot_general | solution.py:81
  145.6 1.6 fusion.51
  147.2 0.7 copy-done.2
  147.9 3.5 %reshape.187 = bf16[5,256,3,128]{1,0,3,2:T(8,128)(2,1)} reshape(bf16[1280,1,384]{0,2,1:T(8,128)(2,1)} %get-tuple-element.135) | data formatting | bytes 1966080 | tf_op jit(solution)/shard_map/while/body/eval_jaxpr/reshape | solution.py:32
  151.4 2.6 copy.22
  153.9 2.2 copy.23
  156.2 1.3 copy.24
  157.5 46.2 %while.19 = (s32[]{:T(128)}, bf16[5,256,3,128]{3,1,2,0:T(8,128)(2,1)}, s32[5]{0:T(128)S(1)}, s32[]{:T(128)}, bf16[5,256,3,128]{3,1,2,0:T(8,128)(2,1)}, /*index=5...) while((s32[]{:T(128)}, ...), condition=%wide.region_5.6_spmd.clone.clone, body=%wide.region_2.5_spmd.clone.clone.sunk | while | flops 764580608 | bytes 4534397 | solution.py:50
  157.5 0.6 dynamic_slice.42
  158.6 0.7 iota_compare_fusion.3
  159.2 0.3 fusion.71
  159.5 2.9 fusion.72
  162.4 4.3 %fusion.73 = bf16[5,256,3,128]{3,1,2,0:T(8,128)(2,1)} fusion(bf16[5,256,3,128]{3,1,2,0:T(8,128)(2,1)} %get-tuple-element.189, s32[]{:T(128)} %get-tuple-element.188, bf16[1280,3,128]{2,0,1:T(8,128)(2,1)} %get-tuple-element.203, f32[3,256]{1,0:T(4,128)S(1)} %fusion.72, bf16[1280,3,128]{2,0,1:T(8,128)(2,1)} %get-tuple-element.202, ...), kind=kOutput, calls=%fused_computation.14.clone.1 | convolution fusion | flops 508332032 | bytes 2691072 | tf_op jit(solution)/shard_map/while/body/eval_jaxpr/while/body/eval_jaxpr/hqk,khe->qhe/dot_general | solution.py:46
  166.7 0.6 dynamic_slice.42
  167.8 0.7 iota_compare_fusion.3
  168.5 0.3 fusion.71
  168.8 2.9 fusion.72
  171.6 4.3 %fusion.73 = bf16[5,256,3,128]{3,1,2,0:T(8,128)(2,1)} fusion(bf16[5,256,3,128]{3,1,2,0:T(8,128)(2,1)} %get-tuple-element.189, s32[]{:T(128)} %get-tuple-element.188, bf16[1280,3,128]{2,0,1:T(8,128)(2,1)} %get-tuple-element.203, f32[3,256]{1,0:T(4,128)S(1)} %fusion.72, bf16[1280,3,128]{2,0,1:T(8,128)(2,1)} %get-tuple-element.202, ...), kind=kOutput, calls=%fused_computation.14.clone.1 | convolution fusion | flops 508332032 | bytes 2691072 | tf_op jit(solution)/shard_map/while/body/eval_jaxpr/while/body/eval_jaxpr/hqk,khe->qhe/dot_general | solution.py:46
  176.0 0.6 dynamic_slice.42
  177.1 0.7 iota_compare_fusion.3
  177.7 0.3 fusion.71
  178.0 2.9 fusion.72
  180.9 4.3 %fusion.73 = bf16[5,256,3,128]{3,1,2,0:T(8,128)(2,1)} fusion(bf16[5,256,3,128]{3,1,2,0:T(8,128)(2,1)} %get-tuple-element.189, s32[]{:T(128)} %get-tuple-element.188, bf16[1280,3,128]{2,0,1:T(8,128)(2,1)} %get-tuple-element.203, f32[3,256]{1,0:T(4,128)S(1)} %fusion.72, bf16[1280,3,128]{2,0,1:T(8,128)(2,1)} %get-tuple-element.202, ...), kind=kOutput, calls=%fused_computation.14.clone.1 | convolution fusion | flops 508332032 | bytes 2691072 | tf_op jit(solution)/shard_map/while/body/eval_jaxpr/while/body/eval_jaxpr/hqk,khe->qhe/dot_general | solution.py:46
  185.2 0.6 dynamic_slice.42
  186.3 0.7 iota_compare_fusion.3
  187.0 0.3 fusion.71
  187.3 2.9 fusion.72
  190.1 4.3 %fusion.73 = bf16[5,256,3,128]{3,1,2,0:T(8,128)(2,1)} fusion(bf16[5,256,3,128]{3,1,2,0:T(8,128)(2,1)} %get-tuple-element.189, s32[]{:T(128)} %get-tuple-element.188, bf16[1280,3,128]{2,0,1:T(8,128)(2,1)} %get-tuple-element.203, f32[3,256]{1,0:T(4,128)S(1)} %fusion.72, bf16[1280,3,128]{2,0,1:T(8,128)(2,1)} %get-tuple-element.202, ...), kind=kOutput, calls=%fused_computation.14.clone.1 | convolution fusion | flops 508332032 | bytes 2691072 | tf_op jit(solution)/shard_map/while/body/eval_jaxpr/while/body/eval_jaxpr/hqk,khe->qhe/dot_general | solution.py:46
  194.4 0.6 dynamic_slice.42
  195.6 0.7 iota_compare_fusion.3
  196.2 0.3 fusion.71
  196.5 2.9 fusion.72
  199.4 4.3 %fusion.73 = bf16[5,256,3,128]{3,1,2,0:T(8,128)(2,1)} fusion(bf16[5,256,3,128]{3,1,2,0:T(8,128)(2,1)} %get-tuple-element.189, s32[]{:T(128)} %get-tuple-element.188, bf16[1280,3,128]{2,0,1:T(8,128)(2,1)} %get-tuple-element.203, f32[3,256]{1,0:T(4,128)S(1)} %fusion.72, bf16[1280,3,128]{2,0,1:T(8,128)(2,1)} %get-tuple-element.202, ...), kind=kOutput, calls=%fused_computation.14.clone.1 | convolution fusion | flops 508332032 | bytes 2691072 | tf_op jit(solution)/shard_map/while/body/eval_jaxpr/while/body/eval_jaxpr/hqk,khe->qhe/dot_general | solution.py:46
  203.7 2.0 copy.25
  205.7 14.1 %convolution_convert_fusion = bf16[1280,6144]{1,0:T(8,128)(2,1)} fusion(bf16[384,6144]{1,0:T(8,128)(2,1)} %param.17, bf16[160,8,3,128]{3,2,1,0:T(4,128)(2,1)S(1)} %bitcast.73), kind=kOutput, calls=%fused_computation.30 | convolution fusion | flops 6047662080 | bytes 21430272 | tf_op jit(solution)/shard_map/dot_general | solution.py:91
  220.5 2.2 gather_fusion
  222.8 3.0 slice_bitcast_fusion
  225.8 4.0 %copy.26 = bf16[2,1280,384]{2,1,0:T(8,128)(2,1)} copy(bf16[2,1280,384]{1,2,0:T(8,128)(2,1)} %slice_bitcast_fusion) | data formatting | bytes 3932160 | tf_op jit(solution)/shard_map/transpose | solution.py:60
  229.8 3.7 %fusion.44 = bf16[10,2,128,384]{3,2,1,0:T(8,128)(2,1)} fusion(bf16[10,2,128,384]{3,2,1,0:T(8,128)(2,1)} %gather_fusion, bf16[2,10,128,384]{3,2,1,0:T(8,128)(2,1)} %bitcast.70, pred[10,128]{1,0:T(8,128)(4,1)S(1)} %add_compare_fusion), kind=kLoop, calls=%fused_computation.43 | loop fusion | flops 983040 | bytes 5899520 | tf_op jit(solution)/shard_map/jit(_where)/select_n | solution.py:70
  233.5 4.5 %scatter_fusion = bf16[2,12,128,384]{3,2,1,0:T(8,128)(2,1)S(1)} fusion(bf16[2,12,128,384]{3,2,1,0:T(8,128)(2,1)S(1)} %copy.47, s32[10]{0:T(128)S(1)} %fusion.47, bf16[10,2,128,384]{3,2,1,0:T(8,128)(2,1)} %fusion.44), kind=kCustom, calls=%fused_computation.1 | custom fusion | bytes 5898280 | tf_op jit(solution)/shard_map/scatter | solution.py:71
  238.0 87.7 %reduce-scatter.2.cloned.1.call-done = bf16[80,6144]{1,0:T(8,128)(2,1)} async-done(((bf16[1280,6144]{1,0:T(8,128)(2,1)}), bf16[80,6144]{1,0:T(8,128)(2,1)}) %reduce-scatter.2.cloned.1.call-update) | async-done | bytes 983056 | tf_op jit(solution)/shard_map/reduce_scatter | solution.py:90
  325.7 2.3 add_convert_fusion
  (33 shorter events, 0.4 us)
Async XLA Ops:
  7.2 1.9 copy-start.1
  7.2 2.6 copy-start.4
  7.2 2.6 copy-start.3
  7.2 112.6 %all-gather.2.cloned.1.call-start = ((), (), s32[]{:S(2)}) async-start(), calls=%async_computation.1 | async-start | bytes 16711680 | tf_op jit(solution)/shard_map/all_gather | solution.py:80
  11.2 314.5 %reduce-scatter.2.cloned.1.call-start = ((), (), s32[]{:S(2)}) async-start(), calls=%async_computation.2 | async-start | bytes 16711680 | tf_op jit(solution)/shard_map/reduce_scatter | solution.py:90
  11.2 18.8 %copy-start.6 = (f32[3,384]{1,0:T(4,128)S(1)}, f32[3,384]{1,0:T(4,128)}, u32[]{:S(2)}) copy-start(f32[3,384]{1,0:T(4,128)} %param.16) | copy-start | bytes 13828
  145.6 2.3 copy-start.2
  219.8 0.7 copy-start.7
  233.5 92.2 %copy-start.5 = (f32[6144]{0:T(1024)S(1)}, f32[6144]{0:T(1024)}, u32[]{:S(2)}) copy-start(f32[6144]{0:T(1024)} %param.18) | copy-start | bytes 73732
  238.0 90.0 %copy-start = (bf16[2,12,128,384]{3,2,1,0:T(8,128)(2,1)}, bf16[2,12,128,384]{3,2,1,0:T(8,128)(2,1)S(1)}, u32[]{:S(2)}) copy-start(bf16[2,12,128,384]{3,2,1,0:T(8,128)(2,1)S(1)} %scatter_fusion) | copy-start | bytes 7077892
Sparse Core Ops, SparseCore 0:
  11.3 108.4 all-gather.1
  219.9 105.7 reduce-scatter.1
where the time goes:
time: 336 us; the launch traced here: 335 us
  waiting for transfers between devices  177 us (53%)
  matrix products  75.7 us (23%)
  local copies, waits for them, and re-layouts  51 us (15%)
  between operations  14.8 us (4%)
  other arithmetic  12.9 us (4%)
    all_gather x1, waiting for transfers between devices, body(): block_rows = lax.all_gather(normed, 'tp', axis=0, tiled=True)  89.7 us
    reduce_scatter x1, waiting for transfers between devices, body(): lax.psum_scatter(jnp.dot(attended, w_out, preferred_element_type=jnp.floa...  87.7 us
    unnamed x21, local copies, waits for them, and re-layouts  27.4 us
    dot_general x1, matrix products, body(): jnp.dot(block_rows, weights_flat, preferred_element_type=jnp.float32)  25.8 us
    dot_general x5, matrix products, one_block(): jnp.einsum('hqk,khe->qhe', weights, seq_value, preferred_element_type=jnp...  21.6 us
    sub x5, matrix products, one_block(): raised = jnp.exp(scores - row_max)  14.3 us
    dot_general x1, matrix products, body(): jnp.dot(attended, w_out, preferred_element_type=jnp.float32)  14.1 us
    transpose x2, local copies, waits for them, and re-layouts, write_cache(): jnp.moveaxis(key_value, 1, 0)  6.97 us
  transfers between devices with their start and end apart: 2, of which 2 were waited for; matrix products, arithmetic and copies ran while one was open for 11% of the time, Pallas kernels for 0%

commit v1 on v0

v1 whole, which is shorter than its diff:
```python
import functools

import jax
import jax.numpy as jnp
from jax import lax
from jax.experimental import pallas as pl
from jax.experimental.pallas import tpu as pltpu
from jax.sharding import PartitionSpec as P

HD = 128
EPS = 1e-05
MESH = pl.DeviceIdType.MESH
RINGS = 4
SUBS = 3
N = 16
ROWS = 80
CW = 512
QW = SUBS * CW
D = RINGS * QW
LEN = N * ROWS
F = 384
HEADS = F // HD
BQ = 256
BATCH = 4
SCALE2 = 1.4426950408889634 / (HD ** 0.5)


def ring_tp(ring, pos):
    a = lax.div(pos, 4)
    b = lax.rem(lax.rem(pos, 4) - a + 4, 4)
    return jnp.where(ring < 2, a * 4 + b, b * 4 + a)


def my_pos(ring, z, x):
    t = lax.rem(z + x, 4)
    return jnp.where(ring < 2, 4 * z + t, 4 * x + t)


def behind(ring, pos, k):
    up = lax.rem(ring, 2)
    return lax.rem(jnp.where(up == 0, pos + N - k, pos + k), N)


def main_kernel(
    len_ref, tok_ref, gain_ref, shift_ref, w_hbm, bq_ref, wo_hbm, bo_ref,
    out_ref, kv_hbm,
    ag, w, acc, qkv, att, wo, rs,
    ag_send, ag_recv, rs_send, rs_recv, w_sem, wo_sem, kv_sem,
):
    tp = lax.axis_index("tp")
    z = lax.div(tp, 4)
    x = lax.rem(tp, 4)
    pos = [my_pos(jnp.int32(r), z, x) for r in range(RINGS)]
    nxt = [ring_tp(jnp.int32(r), behind(jnp.int32(r), pos[r], N - 1)) for r in range(RINGS)]

    barrier = pltpu.get_barrier_semaphore()
    for r in range(RINGS):
        pl.semaphore_signal(barrier, inc=1, device_id={"tp": nxt[r]}, device_id_type=MESH)

    w_copies = [
        pltpu.make_async_copy(w_hbm.at[c], w.at[:, pl.ds(c * F, F)], w_sem.at[c]) for c in range(3)
    ]
    for copy in w_copies:
        copy.start()
    wo_copy = pltpu.make_async_copy(wo_hbm, wo, wo_sem)
    wo_copy.start()

    def norm_rows(i, carry):
        rows = pl.ds(pl.multiple_of(i * 16, 16), 16)
        v = tok_ref[rows, :].astype(jnp.float32)
        center = jnp.mean(v, axis=-1, keepdims=True)
        v = v - center
        spread = jnp.mean(v * v, axis=-1, keepdims=True)
        v = (v * lax.rsqrt(spread + EPS) * gain_ref[...] + shift_ref[...]).astype(jnp.bfloat16)
        for r in range(RINGS):
            for c in range(SUBS):
                ag[r, c, rows, :] = v[:, r * QW + c * CW : r * QW + (c + 1) * CW]
        return carry

    lax.fori_loop(0, ROWS // 16, norm_rows, 0)

    pl.semaphore_wait(barrier, RINGS)

    def slot(s):
        if isinstance(s, int):
            return pl.ds(s * ROWS, ROWS)
        return pl.ds(pl.multiple_of(s * ROWS, 16), ROWS)

    def ag_copy(r, c, s):
        return pltpu.make_async_remote_copy(
            src_ref=ag.at[r, c, slot(s)],
            dst_ref=ag.at[r, c, slot(s + 1)],
            send_sem=ag_send.at[r, c],
            recv_sem=ag_recv.at[r, c, s + 1],
            device_id={"tp": nxt[r]},
            device_id_type=MESH,
        )

    def ag_arrived(r, c, s):
        return pltpu.make_async_remote_copy(
            src_ref=ag.at[r, c, slot(s)],
            dst_ref=ag.at[r, c, slot(s)],
            send_sem=ag_send.at[r, c],
            recv_sem=ag_recv.at[r, c, s],
            device_id={"tp": nxt[r]},
            device_id_type=MESH,
        )

    for c in range(SUBS):
        for r in range(RINGS):
            ag_copy(r, c, 0).start()

    acc[...] = jnp.broadcast_to(bq_ref[...], acc.shape)
    for copy in w_copies:
        copy.wait()

    def unit(b, r, c):
        home = jnp.where(r < 2, 4 * z, 4 * x) + lax.rem(z + x, 4)
        a = ag[r, c, pl.ds(pl.multiple_of(b * (BATCH * ROWS), 64), BATCH * ROWS), :]
        wrow = pl.ds(pl.multiple_of(r * QW + c * CW, CW), CW)
        for lo, hi in ((0, 640), (640, 1152)):
            res = jnp.dot(a, w[wrow, lo:hi], preferred_element_type=jnp.float32)
            for i in range(BATCH):
                src = ring_tp(r, behind(r, home, b * BATCH + i))
                rows = pl.ds(pl.multiple_of(src * ROWS, 16), ROWS)
                acc[rows, lo:hi] += res[i * ROWS : (i + 1) * ROWS]

    def ag_step(s, carry):
        for c in range(SUBS):
            for r in range(RINGS):
                ag_arrived(r, c, s).wait_recv()
                ag_copy(r, c, s - 1).wait_send()
                ag_copy(r, c, s).start()

            @pl.when(s >= BATCH)
            def _():
                u = s - BATCH
                unit(lax.div(u, RINGS), lax.rem(u, RINGS), c)

        return carry

    lax.fori_loop(1, N - 1, ag_step, 0)
    for c in range(SUBS):
        for r in range(RINGS):
            ag_arrived(r, c, N - 1).wait_recv()
            ag_copy(r, c, N - 2).wait_send()

    def tail(u, carry):
        for c in range(SUBS):
            unit(lax.div(u, RINGS), lax.rem(u, RINGS), c)
        return carry

    lax.fori_loop(N - 1 - BATCH, N, tail, 0)

    def to_bf16(i, carry):
        rows = pl.ds(pl.multiple_of(i * 64, 64), 64)
        qkv[rows, :] = acc[rows, :].astype(jnp.bfloat16)
        return carry

    lax.fori_loop(0, LEN // 64, to_bf16, 0)
    kv_copy = pltpu.make_async_copy(qkv.at[:, pl.ds(F, 2 * F)], kv_hbm, kv_sem)
    kv_copy.start()

    last = len_ref[0] - 1

    def head(h, carry):
        col = pl.multiple_of(h * HD, HD)
        for qi in range(LEN // BQ):
            kv = (qi + 1) * BQ
            q = qkv[qi * BQ : (qi + 1) * BQ, pl.ds(col, HD)]
            k = qkv[0:kv, pl.ds(F + col, HD)]
            v = qkv[0:kv, pl.ds(2 * F + col, HD)]
            sc = lax.dot_general(q, k, (((1,), (1,)), ((), ())), preferred_element_type=jnp.float32)
            limit = jnp.minimum(lax.broadcasted_iota(jnp.int32, (BQ, 1), 0) + qi * BQ, last)
            sc = jnp.where(lax.broadcasted_iota(jnp.int32, (BQ, kv), 1) <= limit, sc, -1e30)
            top = jnp.max(sc, axis=-1, keepdims=True)
            e = jnp.exp2((sc - top) * SCALE2)
            inv = 1.0 / jnp.sum(e, axis=-1, keepdims=True)
            p = (e * inv).astype(jnp.bfloat16)
            o = jnp.dot(p, v, preferred_element_type=jnp.float32)
            att[qi * BQ : (qi + 1) * BQ, pl.ds(col, HD)] = o.astype(jnp.bfloat16)
        return carry

    lax.fori_loop(0, HEADS, head, 0)
    wo_copy.wait()

    def partial(r, c, s):
        src = ring_tp(jnp.int32(r), behind(jnp.int32(r), pos[r], s + 1))
        rows = pl.ds(pl.multiple_of(src * ROWS, 16), ROWS)
        lo = r * QW + c * CW
        return jnp.dot(att[rows, :], wo[:, lo : lo + CW], preferred_element_type=jnp.float32)

    def rs_copy(r, c, s):
        return pltpu.make_async_remote_copy(
            src_ref=rs.at[r, c, slot(s)],
            dst_ref=rs.at[r, c, slot(s + 1)],
            send_sem=rs_send.at[r, c],
            recv_sem=rs_recv.at[r, c, s + 1],
            device_id={"tp": nxt[r]},
            device_id_type=MESH,
        )

    def rs_arrived(r, c, s):
        return pltpu.make_async_remote_copy(
            src_ref=rs.at[r, c, slot(s)],
            dst_ref=rs.at[r, c, slot(s)],
            send_sem=rs_send.at[r, c],
            recv_sem=rs_recv.at[r, c, s],
            device_id={"tp": nxt[r]},
            device_id_type=MESH,
        )

    for c in range(SUBS):
        for r in range(RINGS):
            rs[r, c, slot(0), :] = partial(r, c, 0).astype(jnp.bfloat16)
            rs_copy(r, c, 0).start()

    def rs_step(s, carry):
        for c in range(SUBS):
            for r in range(RINGS):
                own = partial(r, c, s)
                rs_arrived(r, c, s).wait_recv()
                rs[r, c, slot(s), :] = (rs[r, c, slot(s), :].astype(jnp.float32) + own).astype(jnp.bfloat16)
                rs_copy(r, c, s - 1).wait_send()
                rs_copy(r, c, s).start()
        return carry

    lax.fori_loop(1, N - 1, rs_step, 0)
    for c in range(SUBS):
        for r in range(RINGS):
            lo = r * QW + c * CW
            own = partial(r, c, N - 1) + bo_ref[:, lo : lo + CW]
            rs_arrived(r, c, N - 1).wait_recv()
            rs_copy(r, c, N - 2).wait_send()
            out_ref[:, lo : lo + CW] = (rs[r, c, slot(N - 1), :].astype(jnp.float32) + own).astype(jnp.bfloat16)
    kv_copy.wait()


def cache_kernel(page_ref, len_ref, old_ref, new_ref, out_ref):
    page = page_ref[pl.program_id(0)]
    row = lax.broadcasted_iota(jnp.int32, (128, 1), 0) + page * 128
    written = (row < len_ref[0]) & (row >= 0)
    for i in range(2):
        out_ref[i, 0] = jnp.where(written, new_ref[:, i * F : (i + 1) * F], old_ref[i, 0])


def body(tokens, ln_gain, ln_bias, w_qkv, b_qkv, w_out, b_out, kv_cache, page_table, lengths):
    vmem = pl.BlockSpec(memory_space=pltpu.VMEM)
    anym = pl.BlockSpec(memory_space=pl.ANY)
    out, kv_new = pl.pallas_call(
        main_kernel,
        out_shape=(
            jax.ShapeDtypeStruct((ROWS, D), jnp.bfloat16),
            jax.ShapeDtypeStruct((LEN, 2 * F), jnp.bfloat16),
        ),
        in_specs=[pl.BlockSpec(memory_space=pltpu.SMEM), vmem, vmem, vmem, anym, vmem, anym, vmem],
        out_specs=(vmem, anym),
        scratch_shapes=[
            pltpu.VMEM((RINGS, SUBS, LEN, CW), jnp.bfloat16),
            pltpu.VMEM((D, 3 * F), jnp.bfloat16),
            pltpu.VMEM((LEN, 3 * F), jnp.float32),
            pltpu.VMEM((LEN, 3 * F), jnp.bfloat16),
            pltpu.VMEM((LEN, F), jnp.bfloat16),
            pltpu.VMEM((F, D), jnp.bfloat16),
            pltpu.VMEM((RINGS, SUBS, LEN, CW), jnp.bfloat16),
            pltpu.SemaphoreType.DMA((RINGS, SUBS)),
            pltpu.SemaphoreType.DMA((RINGS, SUBS, N)),
            pltpu.SemaphoreType.DMA((RINGS, SUBS)),
            pltpu.SemaphoreType.DMA((RINGS, SUBS, N)),
            pltpu.SemaphoreType.DMA((3,)),
            pltpu.SemaphoreType.DMA,
            pltpu.SemaphoreType.DMA,
        ],
        compiler_params=pltpu.CompilerParams(
            collective_id=0, has_side_effects=True, vmem_limit_bytes=67043328
        ),
        name="sublayer",
    )(
        lengths,
        tokens,
        ln_gain.reshape(1, D),
        ln_bias.reshape(1, D),
        jnp.transpose(w_qkv, (1, 0, 2)),
        b_qkv.reshape(1, 3 * F),
        w_out,
        b_out.reshape(1, D),
    )

    slots = kv_cache.shape[1]
    hit = page_table.reshape(1, -1) == jnp.arange(slots, dtype=jnp.int32)[:, None]
    pages = jnp.arange(page_table.size, dtype=jnp.int32)[None]
    page_of = jnp.max(jnp.where(hit, pages, -1), axis=1)
    kv_out = pl.pallas_call(
        cache_kernel,
        out_shape=jax.ShapeDtypeStruct(kv_cache.shape, kv_cache.dtype),
        grid_spec=pltpu.PrefetchScalarGridSpec(
            num_scalar_prefetch=2,
            grid=(slots,),
            in_specs=[
                pl.BlockSpec((2, 1, 128, F), lambda i, page, n: (0, i, 0, 0)),
                pl.BlockSpec((128, 2 * F), lambda i, page, n: (jnp.maximum(page[i], 0), 0)),
            ],
            out_specs=pl.BlockSpec((2, 1, 128, F), lambda i, page, n: (0, i, 0, 0)),
        ),
        name="cache_write",
    )(page_of, lengths, kv_cache, kv_new)
    return out, kv_out


def solution(mesh):
    placed = (
        P(("dp", "tp"), None),
        P(),
        P(),
        P(None, None, "tp"),
        P(None, "tp"),
        P("tp", None),
        P(),
        P(None, "dp", None, "tp"),
        P("dp", None),
        P("dp"),
    )
    return jax.shard_map(
        body,
        mesh=mesh,
        in_specs=placed,
        out_specs=(P(("dp", "tp"), None), P(None, "dp", None, "tp")),
        check_vma=False,
    )
```

time: 336 us -> 206 us (0.61)
  Pallas kernels: 0 us -> 201 us
  waiting for transfers between devices: 177 us -> 0 us
  matrix products: 75.7 us -> 0 us
  local copies, waits for them, and re-layouts: 51 us -> 2.24 us
  between operations: 14.8 us -> 1.29 us
  other arithmetic: 12.9 us -> 1.28 us
    pallas_call x0 -> x2, Pallas kernels: none -> 201 us  [the longest x1 192 us: body(): pl.pallas_call(main_kernel, out_shape=(jax.ShapeDtypeStruct((ROWS, D), jn...]
    all_gather x1 -> x0, waiting for transfers between devices: 89.7 us -> none  [body(): block_rows = lax.all_gather(normed, 'tp', axis=0, tiled=True)]
    reduce_scatter x1 -> x0, waiting for transfers between devices: 87.7 us -> none  [body(): lax.psum_scatter(jnp.dot(attended, w_out, preferred_element_type=jnp.floa...]
    dot_general x7 -> x0, matrix products: 61.5 us -> none  [the longest x1 25.8 us: body(): jnp.dot(block_rows, weights_flat, preferred_element_type=jnp.float32)]
    unnamed x21 -> x4, local copies, waits for them, and re-layouts: 27.4 us -> 2.24 us
    sub x5 -> x0, matrix products: 14.3 us -> none  [one_block(): raised = jnp.exp(scores - row_max)]
    transpose x2 -> x0, local copies, waits for them, and re-layouts: 6.97 us -> none  [write_cache(): jnp.moveaxis(key_value, 1, 0)]
    scatter x1 -> x0, local copies, waits for them, and re-layouts: 4.47 us -> none  [write_cache(): return kv_cache.at[:, slot_ids].set(new_pages)]
  transfers between devices with their start and end apart: 2 -> 0, of which waited for: 2 -> 0; matrix products, arithmetic and copies ran while one was open for 11% -> 0% of each run, Pallas kernels for 0% -> 0%
where the time goes in v1:
time: 206 us
  Pallas kernels  201 us (98%)
  local copies, waits for them, and re-layouts  2.24 us (1%)
    pallas_call x1, Pallas kernels, body(): pl.pallas_call(main_kernel, out_shape=(jax.ShapeDtypeStruct((ROWS, D), jn...  192 us
    pallas_call x1, Pallas kernels, body(): pl.pallas_call(cache_kernel, out_shape=jax.ShapeDtypeStruct(kv_cache.shap...  9.09 us

profile of v1, /device:TPU:0, one launch (start us, length us, event | category | flops | bytes accessed | tf_op | source)
XLA Modules:
  0.0 205.6 jit_solution(7107111505102588521)
XLA Ops:
  1.3 1.3 select_reduce_fusion.page_ref
  2.6 1.3 copy.12
  3.8 191.7 %sublayer.1 = (bf16[80,6144]{1,0:T(8,128)(2,1)}, bf16[1280,768]{1,0:T(8,128)(2,1)}) custom-call(s32[1]{0:T(128)S(6)} %copy.14.len_ref, bf16[80,6144]{1,0:T(8,128)(2,1)} %tok_ref.1, f32[1,6144]{1,0:T(1,128)} %bitcast.9, f32[1,6144]{1,0:T(1,128)} %bitcast.10, bf16[3,6144,384]{2,1,0:T(8,128)(2,1)} %bitcast.8, f32[1,1152]{1,0:T(1,128)} %bitcast.12, ...), custom_call_target="tpu_custom_call" | custom-call | tf_op jit(solution)/shard_map/sublayer/pallas_call | solution.py:250
  195.6 0.0 copy-start
  195.6 9.1 %cache_write.1 = bf16[2,12,128,384]{3,2,1,0:T(8,128)(2,1)} custom-call(s32[12]{0:T(128)} %select_reduce_fusion.page_ref, s32[1]{0:T(128)S(6)} %copy.14.len_ref, bf16[2,12,128,384]{3,2,1,0:T(8,128)(2,1)} %old_ref.1, bf16[1280,768]{1,0:T(8,128)(2,1)} %get-tuple-element.5.new_ref), custom_call_target="tpu_custom_call" | custom-call | tf_op jit(solution)/shard_map/cache_write/pallas_call | solution.py:293
  204.6 0.0 copy-done
  204.7 0.9 copy.15
Async XLA Ops:
  195.6 9.1 %copy-start = (bf16[80,6144]{1,0:T(8,128)(2,1)S(1)}, bf16[80,6144]{1,0:T(8,128)(2,1)}, u32[]{:S(2)}) copy-start(bf16[80,6144]{1,0:T(8,128)(2,1)} %get-tuple-element.8) | copy-start | bytes 2949124

commit v2 on v1

v2 whole, which is shorter than its diff:
```python
import functools

import jax
import jax.numpy as jnp
from jax import lax
from jax.experimental import pallas as pl
from jax.experimental.pallas import tpu as pltpu
from jax.sharding import PartitionSpec as P

HD = 128
EPS = 1e-05
MESH = pl.DeviceIdType.MESH
RINGS = 4
SUBS = 3
N = 16
ROWS = 80
CW = 512
QW = SUBS * CW
D = RINGS * QW
LEN = N * ROWS
F = 384
HEADS = F // HD
BQ = 320
BATCH = 4
PAGE = 128
PAGES = LEN // PAGE
SLOTS = 12
HC = D // 2
PR = F // 8
KX = 4 * F
CHUNKS = 12
LAG = 4
FORWARD_AT = 4
SCALE2 = 1.4426950408889634 / (HD ** 0.5)


def ring_tp(ring, pos):
    a = lax.div(pos, 4)
    b = lax.rem(lax.rem(pos, 4) - a + 4, 4)
    return jnp.where(ring < 2, a * 4 + b, b * 4 + a)


def my_pos(ring, z, x):
    t = lax.rem(z + x, 4)
    return jnp.where(ring < 2, 4 * z + t, 4 * x + t)


def behind(ring, pos, k):
    up = lax.rem(ring, 2)
    return lax.rem(jnp.where(up == 0, pos + N - k, pos + k), N)


def main_kernel(
    len_ref, page_ref, tok_ref, gain_ref, shift_ref, w_hbm, bq_ref, wo_hbm, bo_ref, old_hbm,
    out_ref, kv_hbm, g_hbm,
    ag, w, acc, qkv, att, wx, gat, psend, prec,
    ag_send, ag_recv, w_sem, kv_sem,
    g1_send, g1_recv, g2_send, g2_recv, gy_send, gy_recv, gf_send, gf_recv, gd_send, gd_recv,
    l_sem, at_send, at_recv, p_send, p_recv,
):
    tp = lax.axis_index("tp")
    dp = lax.axis_index("dp")
    z = lax.div(tp, 4)
    x = lax.rem(tp, 4)
    y = lax.div(dp, 2)
    core = lax.rem(dp, 2)
    pos = [my_pos(jnp.int32(r), z, x) for r in range(RINGS)]
    nxt = [ring_tp(jnp.int32(r), behind(jnp.int32(r), pos[r], N - 1)) for r in range(RINGS)]

    def along(axis, j):
        if axis == 0:
            return {"tp": z * 4 + lax.rem(x + j, 4)}
        return {"tp": lax.rem(z + j, 4) * 4 + x}

    def along_y(j):
        return {"dp": lax.rem(y + j, 4) * 2 + core}

    sibling = {"dp": y * 2 + 1 - core}

    barrier = pltpu.get_barrier_semaphore()
    peers = [along(a, j) for a in range(2) for j in (1, 2, 3)] + [along_y(1), along_y(3), sibling]
    for peer in peers:
        pl.semaphore_signal(barrier, inc=1, device_id=peer, device_id_type=MESH)

    w_copies = [
        pltpu.make_async_copy(w_hbm.at[c], w.at[:, pl.ds(c * F, F)], w_sem.at[c]) for c in range(3)
    ]
    for copy in w_copies:
        copy.start()
    pl.semaphore_wait(barrier, len(peers))

    def remote(src, dst, send_sem, recv_sem, device):
        return pltpu.make_async_remote_copy(
            src_ref=src, dst_ref=dst, send_sem=send_sem, recv_sem=recv_sem,
            device_id=device, device_id_type=MESH,
        )

    piece = pl.ds(pl.multiple_of((core * 4 + y) * PR, PR), PR)

    def g1_copy(axis, j):
        return remote(
            wo_hbm.at[piece, pl.ds(axis * HC, HC)], g_hbm.at[axis, 3 - j, piece],
            g1_send.at[axis, 3 - j], g1_recv.at[axis, 3 - j], along(axis, j),
        )

    def g2_copy(axis, j):
        k = 4 - j
        cols = pl.ds(0 if j == 1 else HC // 2, HC // 2)
        return remote(
            g_hbm.at[axis, k - 1, piece, cols], g_hbm.at[axis, 1, piece, cols],
            g2_send.at[axis, 3 - j], g2_recv.at[axis, 3 - j], along(axis, j),
        )

    for axis in range(2):
        for j in (1, 3):
            g1_copy(axis, j).start()

    def norm_rows(i, carry):
        rows = pl.ds(pl.multiple_of(i * 16, 16), 16)
        v = tok_ref[rows, :].astype(jnp.float32)
        center = jnp.mean(v, axis=-1, keepdims=True)
        v = v - center
        spread = jnp.mean(v * v, axis=-1, keepdims=True)
        v = (v * lax.rsqrt(spread + EPS) * gain_ref[...] + shift_ref[...]).astype(jnp.bfloat16)
        for r in range(RINGS):
            for c in range(SUBS):
                ag[r, c, rows, :] = v[:, r * QW + c * CW : r * QW + (c + 1) * CW]
        return carry

    lax.fori_loop(0, ROWS // 16, norm_rows, 0)

    def slot(s):
        if isinstance(s, int):
            return pl.ds(s * ROWS, ROWS)
        return pl.ds(pl.multiple_of(s * ROWS, 16), ROWS)

    def ag_copy(r, c, s):
        return remote(
            ag.at[r, c, slot(s)], ag.at[r, c, slot(s + 1)],
            ag_send.at[r, c], ag_recv.at[r, c, s + 1], {"tp": nxt[r]},
        )

    def ag_arrived(r, c, s):
        return remote(
            ag.at[r, c, slot(s)], ag.at[r, c, slot(s)],
            ag_send.at[r, c], ag_recv.at[r, c, s], {"tp": nxt[r]},
        )

    for r in range(RINGS):
        ag_copy(r, 0, 0).start()
    for j in (1, 3):
        for axis in range(2):
            g1_copy(axis, j).wait_recv()
            g2_copy(axis, j).start()
    for c in range(1, SUBS):
        for r in range(RINGS):
            ag_copy(r, c, 0).start()

    for c in range(3):
        acc[:, c * F : (c + 1) * F] = jnp.broadcast_to(bq_ref[c : c + 1, :], (LEN, F))
    for copy in w_copies:
        copy.wait()

    def gy_copy(axis, k, j):
        return remote(
            g_hbm.at[axis, k - 1, piece], g_hbm.at[axis, k - 1, piece],
            gy_send.at[axis, k - 1, j // 2], gy_recv.at[axis, k - 1, j // 2], along_y(j),
        )

    def gf_copy(axis, k):
        j = 1 if axis == 0 else 3
        src = pl.ds(pl.multiple_of((core * 4 + lax.rem(y + 4 - j, 4)) * PR, PR), PR)
        return remote(
            g_hbm.at[axis, k - 1, src], g_hbm.at[axis, k - 1, src],
            gf_send.at[axis, k - 1], gf_recv.at[axis, k - 1], along_y(j),
        )

    for k in (1, 3, 2):
        if k == 2:
            for axis in range(2):
                for j in (1, 3):
                    g2_copy(axis, j).wait_recv()
        for axis in range(2):
            gy_copy(axis, k, 1 if axis == 0 else 3).start()
    for k in (1, 3, 2):
        for axis in range(2):
            gy_copy(axis, k, 3 if axis == 0 else 1).start()

    def unit(b, r, c):
        home = jnp.where(r < 2, 4 * z, 4 * x) + lax.rem(z + x, 4)
        a = ag[r, c, pl.ds(pl.multiple_of(b * (BATCH * ROWS), 64), BATCH * ROWS), :]
        wrow = pl.ds(pl.multiple_of(r * QW + c * CW, CW), CW)
        for lo, hi in ((0, 640), (640, 1152)):
            res = jnp.dot(a, w[wrow, lo:hi], preferred_element_type=jnp.float32)
            for i in range(BATCH):
                src = ring_tp(r, behind(r, home, b * BATCH + i))
                rows = pl.ds(pl.multiple_of(src * ROWS, 16), ROWS)
                acc[rows, lo:hi] += res[i * ROWS : (i + 1) * ROWS]

    def ag_step(s, carry):
        for c in range(SUBS):
            for r in range(RINGS):
                ag_arrived(r, c, s).wait_recv()
                ag_copy(r, c, s - 1).wait_send()
                ag_copy(r, c, s).start()

            @pl.when(s >= BATCH)
            def _():
                u = s - BATCH
                unit(lax.div(u, RINGS), lax.rem(u, RINGS), c)

        for i, k in enumerate((1, 3, 2)):

            @pl.when(s == FORWARD_AT + i)
            def _():
                for axis in range(2):
                    gy_copy(axis, k, 1 if axis == 0 else 3).wait_recv()
                    gf_copy(axis, k).start()

        return carry

    lax.fori_loop(1, N - 1, ag_step, 0)
    for c in range(SUBS):
        for r in range(RINGS):
            ag_arrived(r, c, N - 1).wait_recv()
            ag_copy(r, c, N - 2).wait_send()

    mine = pl.ds(pl.multiple_of(core * (4 * PR), 4 * PR), 4 * PR)

    def gd_copy(axis, k):
        return remote(
            g_hbm.at[axis, k - 1, mine], g_hbm.at[axis, k - 1, mine],
            gd_send.at[axis, k - 1], gd_recv.at[axis, k - 1], sibling,
        )

    blocks = [(axis, k) for axis in range(2) for k in (1, 2, 3)]
    for axis, k in blocks:
        gy_copy(axis, k, 3 if axis == 0 else 1).wait_recv()
        gf_copy(axis, k).wait_recv()
        gd_copy(axis, k).start()

    def tail(u, carry):
        for c in range(SUBS):
            unit(lax.div(u, RINGS), lax.rem(u, RINGS), c)
        return carry

    lax.fori_loop(N - 1 - BATCH, N, tail, 0)

    def to_bf16(i, carry):
        rows = pl.ds(pl.multiple_of(i * 64, 64), 64)
        qkv[rows, :] = acc[rows, :].astype(jnp.bfloat16)
        return carry

    lax.fori_loop(0, LEN // 64, to_bf16, 0)

    half = SLOTS * PAGE // 2
    old_copies = [
        pltpu.make_async_copy(
            old_hbm.at[i, pl.ds(p * half, half)], ag.at[p, i, pl.ds(0, half), pl.ds(0, F)], kv_sem.at[p, i]
        )
        for p in range(2) for i in range(2)
    ]
    kv_copies = [
        pltpu.make_async_copy(
            ag.at[p, i, pl.ds(0, half), pl.ds(0, F)], kv_hbm.at[i, pl.ds(p * half, half)], kv_sem.at[p, i]
        )
        for p in range(2) for i in range(2)
    ]
    for copy in old_copies:
        copy.start()

    def home_of(n):
        if n < 8:
            return w, (n // 2) * KX, (n % 2) * CW
        return wx, 0, (n - 8) * CW

    def load(n, k):
        axis, m = n % 2, n // 2
        ref, row, col = home_of(n)
        if k == 0:
            src = wo_hbm.at[:, pl.ds(axis * HC + m * CW, CW)]
        else:
            src = g_hbm.at[axis, k - 1, :, pl.ds(m * CW, CW)]
        return pltpu.make_async_copy(src, ref.at[pl.ds(row + k * F, F), pl.ds(col, CW)], l_sem.at[n, k])

    for axis, k in blocks:
        gd_copy(axis, k).wait_recv()
    for n in range(CHUNKS):
        for k in range(4):
            load(n, k).start()

    last = len_ref[0] - 1

    def at_copy(axis, h, j):
        cols = pl.ds(pl.multiple_of(h * HD, HD), HD)
        there = pl.ds(pl.multiple_of((4 - j) * F + h * HD, HD), HD)
        if axis == 0:
            src = att.at[:, lax.rem(x + j, 4), :, cols]
        else:
            src = att.at[lax.rem(z + j, 4), :, :, cols]
        return remote(
            src, gat.at[axis, :, :, there], at_send.at[axis, h, j - 1], at_recv.at[axis, h, 3 - j],
            along(axis, j),
        )

    def head(h, carry):
        col = pl.multiple_of(h * HD, HD)
        for qi in range(LEN // BQ):
            kv = -(-(qi + 1) * BQ // HD) * HD
            q = qkv[qi * BQ : (qi + 1) * BQ, pl.ds(col, HD)]
            k = qkv[0:kv, pl.ds(F + col, HD)]
            v = qkv[0:kv, pl.ds(2 * F + col, HD)]
            sc = lax.dot_general(q, k, (((1,), (1,)), ((), ())), preferred_element_type=jnp.float32)
            limit = jnp.minimum(lax.broadcasted_iota(jnp.int32, (BQ, 1), 0) + qi * BQ, last)
            sc = jnp.where(lax.broadcasted_iota(jnp.int32, (BQ, kv), 1) <= limit, sc, -1e30)
            top = jnp.max(sc, axis=-1, keepdims=True)
            e = jnp.exp2((sc - top) * SCALE2)
            inv = 1.0 / jnp.sum(e, axis=-1, keepdims=True)
            p = (e * inv).astype(jnp.bfloat16)
            o = jnp.dot(p, v, preferred_element_type=jnp.float32)
            att[qi, :, :, pl.ds(col, HD)] = o.astype(jnp.bfloat16).reshape(4, ROWS, HD)
        for j in (2, 1, 3):
            for axis in range(2):
                at_copy(axis, h, j).start()
        return carry

    lax.fori_loop(0, HEADS, head, 0)
    for b in range(4):
        gat[0, b, :, 0:F] = att[b, x]
        gat[1, b, :, 0:F] = att[z, b]

    for copy in old_copies:
        copy.wait()

    def merge_slot(i, carry):
        plane, rows = lax.div(i, 6), pl.ds(pl.multiple_of(lax.rem(i, 6) * PAGE, PAGE), PAGE)
        row = lax.broadcasted_iota(jnp.int32, (PAGE, F), 0)
        for c in range(2):
            merged = ag[plane, c, rows, 0:F]
            for p in range(PAGES):
                here = (jnp.full((PAGE, F), page_ref[0, p], jnp.int32) == i) & (row + p * PAGE <= last)
                merged = jnp.where(here, qkv[p * PAGE : (p + 1) * PAGE, (1 + c) * F : (2 + c) * F], merged)
            ag[plane, c, rows, 0:F] = merged
        return carry

    lax.fori_loop(0, SLOTS, merge_slot, 0)
    for h in range(HEADS):
        for j in (1, 2, 3):
            for axis in range(2):
                at_copy(axis, h, j).wait_recv()
    for copy in kv_copies:
        copy.start()

    def p_copy(n, what):
        axis, ahead = 1 - n % 2, (1 if (n // 2) % 2 == 0 else 3)
        here = x if axis == 0 else z
        j = 4 - ahead if what == 2 else ahead
        block = lax.rem(here + (2 if what == 0 else j), 4)
        return remote(
            psend.at[n, block], prec.at[n, what], p_send.at[n, what], p_recv.at[n, what], along(axis, j)
        )

    def p_add(n):
        axis, ahead = 1 - n % 2, (1 if (n // 2) % 2 == 0 else 3)
        block = lax.rem((x if axis == 0 else z) + ahead, 4)
        p_copy(n, 0).wait_recv()
        both = psend[n, block].astype(jnp.float32) + prec[n, 0].astype(jnp.float32)
        psend[n, block] = both.astype(jnp.bfloat16)
        p_copy(n, 1).start()

    for n in range(CHUNKS):
        ref, row, col = home_of(n)
        for k in range(4):
            load(n, k).wait()
        a = gat[n % 2].reshape(4 * ROWS, KX)
        res = jnp.dot(a, ref[row : row + KX, col : col + CW], preferred_element_type=jnp.float32)
        psend[n] = res.astype(jnp.bfloat16).reshape(4, ROWS, CW)
        p_copy(n, 0).start()
        p_copy(n, 2).start()
        if n >= LAG:
            p_add(n - LAG)
    for n in range(CHUNKS - LAG, CHUNKS):
        p_add(n)

    for n in range(CHUNKS):
        here = z if n % 2 == 0 else x
        lo = (n % 2) * HC + (n // 2) * CW
        total = psend[n, here].astype(jnp.float32) + bo_ref[:, lo : lo + CW]
        p_copy(n, 2).wait_recv()
        total += prec[n, 2].astype(jnp.float32)
        p_copy(n, 1).wait_recv()
        total += prec[n, 1].astype(jnp.float32)
        out_ref[:, lo : lo + CW] = total.astype(jnp.bfloat16)

    for n in range(CHUNKS):
        for what in range(3):
            p_copy(n, what).wait_send()
    for axis in range(2):
        for j in (1, 3):
            g1_copy(axis, j).wait_send()
            g2_copy(axis, j).wait_send()
        for k in (1, 2, 3):
            gy_copy(axis, k, 1).wait_send()
            gy_copy(axis, k, 3).wait_send()
            gf_copy(axis, k).wait_send()
            gd_copy(axis, k).wait_send()
        for h in range(HEADS):
            for j in (1, 2, 3):
                at_copy(axis, h, j).wait_send()
    for copy in kv_copies:
        copy.wait()


def body(tokens, ln_gain, ln_bias, w_qkv, b_qkv, w_out, b_out, kv_cache, page_table, lengths):
    vmem = pl.BlockSpec(memory_space=pltpu.VMEM)
    anym = pl.BlockSpec(memory_space=pl.ANY)
    smem = pl.BlockSpec(memory_space=pltpu.SMEM)
    dma = pltpu.SemaphoreType.DMA
    out, kv_out, _ = pl.pallas_call(
        main_kernel,
        out_shape=(
            jax.ShapeDtypeStruct((ROWS, D), jnp.bfloat16),
            jax.ShapeDtypeStruct((2, SLOTS * PAGE, F), jnp.bfloat16),
            jax.ShapeDtypeStruct((2, 3, F, HC), jnp.bfloat16),
        ),
        in_specs=[smem, smem, vmem, vmem, vmem, anym, vmem, anym, vmem, anym],
        out_specs=(vmem, anym, anym),
        scratch_shapes=[
            pltpu.VMEM((RINGS, SUBS, LEN, CW), jnp.bfloat16),
            pltpu.VMEM((D, 3 * F), jnp.bfloat16),
            pltpu.VMEM((LEN, 3 * F), jnp.float32),
            pltpu.VMEM((LEN, 3 * F), jnp.bfloat16),
            pltpu.VMEM((4, 4, ROWS, F), jnp.bfloat16),
            pltpu.VMEM((KX, 4 * CW), jnp.bfloat16),
            pltpu.VMEM((2, 4, ROWS, KX), jnp.bfloat16),
            pltpu.VMEM((CHUNKS, 4, ROWS, CW), jnp.bfloat16),
            pltpu.VMEM((CHUNKS, 3, ROWS, CW), jnp.bfloat16),
            dma((RINGS, SUBS)),
            dma((RINGS, SUBS, N)),
            dma((3,)),
            dma((2, 2)),
            dma((2, 3)),
            dma((2, 3)),
            dma((2, 3)),
            dma((2, 3)),
            dma((2, 3, 2)),
            dma((2, 3, 2)),
            dma((2, 3)),
            dma((2, 3)),
            dma((2, 3)),
            dma((2, 3)),
            dma((CHUNKS, 4)),
            dma((2, HEADS, 3)),
            dma((2, HEADS, 3)),
            dma((CHUNKS, 3)),
            dma((CHUNKS, 3)),
        ],
        compiler_params=pltpu.CompilerParams(
            collective_id=0, has_side_effects=True, vmem_limit_bytes=67043328
        ),
        name="sublayer",
    )(
        lengths,
        page_table,
        tokens,
        ln_gain.reshape(1, D),
        ln_bias.reshape(1, D),
        jnp.transpose(w_qkv, (1, 0, 2)),
        b_qkv,
        w_out,
        b_out.reshape(1, D),
        kv_cache.reshape(2, SLOTS * PAGE, F),
    )
    return out, kv_out.reshape(kv_cache.shape)


def solution(mesh):
    placed = (
        P(("dp", "tp"), None),
        P(),
        P(),
        P(None, None, "tp"),
        P(None, "tp"),
        P("tp", None),
        P(),
        P(None, "dp", None, "tp"),
        P("dp", None),
        P("dp"),
    )
    return jax.shard_map(
        body,
        mesh=mesh,
        in_specs=placed,
        out_specs=(P(("dp", "tp"), None), P(None, "dp", None, "tp")),
        check_vma=False,
    )
```

time: 206 us -> 159 us (0.77)
  Pallas kernels: 201 us -> 151 us
  local copies, waits for them, and re-layouts: 2.24 us -> 5.63 us
    pallas_call x1, Pallas kernels: 192 us -> 151 us  [body(): pl.pallas_call(main_kernel, out_shape=(jax.ShapeDtypeStruct((ROWS, D), jn...]
    pallas_call x1 -> x0, Pallas kernels: 9.09 us -> none  [body(): pl.pallas_call(cache_kernel, out_shape=jax.ShapeDtypeStruct(kv_cache.shap...]
    unnamed x4 -> x2, local copies, waits for them, and re-layouts: 2.24 us -> 5.63 us
where the time goes in v2:
time: 159 us; the launch traced here: 158 us
  Pallas kernels  151 us (95%)
  local copies, waits for them, and re-layouts  5.63 us (4%)
    pallas_call x1, Pallas kernels, body(): pl.pallas_call(main_kernel, out_shape=(jax.ShapeDtypeStruct((ROWS, D), jn...  151 us
    unnamed x2, local copies, waits for them, and re-layouts  5.63 us

profile of v2, /device:TPU:0, one launch (start us, length us, event | category | flops | bytes accessed | tf_op | source)
XLA Modules:
  0.0 158.2 jit_solution(14522244790154209239)
XLA Ops:
  1.3 151.3 %sublayer.1 = (bf16[80,6144]{1,0:T(8,128)(2,1)}, bf16[2,1536,384]{2,1,0:T(8,128)(2,1)}, bf16[2,3,384,3072]{3,2,1,0:T(8,128)(2,1)}) custom-call(s32[1]{0:T(128)S(6)} %copy.14.len_ref, s32[1,10]{1,0:T(1,128)} %page_ref.1, bf16[80,6144]{1,0:T(8,128)(2,1)} %tok_ref.1, f32[1,6144]{1,0:T(1,128)} %bitcast.9, f32[1,6144]{1,0:T(1,128)} %bitcast.10, ...), custom_call_target="tpu_custom_call" | custom-call | tf_op jit(solution)/shard_map/sublayer/pallas_call | solution.py:419
  152.6 2.2 %copy.15 = bf16[80,6144]{1,0:T(8,128)(2,1)} copy(bf16[80,6144]{1,0:T(8,128)(2,1)} %get-tuple-element.8) | data formatting | bytes 1966080
  154.8 3.4 %copy.16 = bf16[2,12,128,384]{3,2,1,0:T(8,128)(2,1)} copy(bf16[2,12,128,384]{3,2,1,0:T(8,128)(2,1)} %bitcast.8) | data formatting | bytes 4718592

commit v3 on v2

--- a/solution.py
+++ b/solution.py
@@ -30,6 +30,7 @@
 KX = 4 * F
 CHUNKS = 12
 LAG = 4
+DIRECT = 8
 FORWARD_AT = 4
 SCALE2 = 1.4426950408889634 / (HD ** 0.5)
 
@@ -51,12 +52,12 @@
 
 
 def main_kernel(
-    len_ref, page_ref, tok_ref, gain_ref, shift_ref, w_hbm, bq_ref, wo_hbm, bo_ref, old_hbm,
+    len_ref, tok_ref, gain_ref, shift_ref, w_hbm, bq_ref, wo_hbm, bo_ref,
     out_ref, kv_hbm, g_hbm,
     ag, w, acc, qkv, att, wx, gat, psend, prec,
     ag_send, ag_recv, w_sem, kv_sem,
     g1_send, g1_recv, g2_send, g2_recv, gy_send, gy_recv, gf_send, gf_recv, gd_send, gd_recv,
-    l_sem, at_send, at_recv, p_send, p_recv,
+    l_sem, at_send, at_recv, ax_send, ax_recv, p_send, p_recv,
 ):
     tp = lax.axis_index("tp")
     dp = lax.axis_index("dp")
@@ -186,28 +187,46 @@
         for axis in range(2):
             gy_copy(axis, k, 3 if axis == 0 else 1).start()
 
-    def unit(b, r, c):
+    def unit(first, count, r, subs, cols):
         home = jnp.where(r < 2, 4 * z, 4 * x) + lax.rem(z + x, 4)
-        a = ag[r, c, pl.ds(pl.multiple_of(b * (BATCH * ROWS), 64), BATCH * ROWS), :]
-        wrow = pl.ds(pl.multiple_of(r * QW + c * CW, CW), CW)
-        for lo, hi in ((0, 640), (640, 1152)):
-            res = jnp.dot(a, w[wrow, lo:hi], preferred_element_type=jnp.float32)
-            for i in range(BATCH):
-                src = ring_tp(r, behind(r, home, b * BATCH + i))
-                rows = pl.ds(pl.multiple_of(src * ROWS, 16), ROWS)
-                acc[rows, lo:hi] += res[i * ROWS : (i + 1) * ROWS]
+        rows = pl.ds(pl.multiple_of(first * ROWS, 16), count * ROWS)
+        for lo, hi in cols:
+            res = None
+            for c in subs:
+                wrow = pl.ds(pl.multiple_of(r * QW + c * CW, CW), CW)
+                part = jnp.dot(ag[r, c, rows, :], w[wrow, lo:hi], preferred_element_type=jnp.float32)
+                res = part if res is None else res + part
+            for i in range(count):
+                src = ring_tp(r, behind(r, home, first + i))
+                to = pl.ds(pl.multiple_of(src * ROWS, 16), ROWS)
+                acc[to, lo:hi] += res[i * ROWS : (i + 1) * ROWS]
+
+    halves, whole = ((0, 640), (640, 1152)), ((0, 1152),)
+
+    mine = pl.ds(pl.multiple_of(core * (4 * PR), 4 * PR), 4 * PR)
+
+    def gd_copy(axis, k):
+        return remote(
+            g_hbm.at[axis, k - 1, mine], g_hbm.at[axis, k - 1, mine],
+            gd_send.at[axis, k - 1], gd_recv.at[axis, k - 1], sibling,
+        )
+
+    blocks = [(axis, k) for axis in range(2) for k in (1, 2, 3)]
 
     def ag_step(s, carry):
+        first = jnp.where(s < 12, s - 4, 2 * s - 16)
+        count = jnp.where(s < 4, 0, jnp.where(s < 12, 1, jnp.where(s < 14, 2, 0)))
         for c in range(SUBS):
             for r in range(RINGS):
                 ag_arrived(r, c, s).wait_recv()
                 ag_copy(r, c, s - 1).wait_send()
                 ag_copy(r, c, s).start()
 
-            @pl.when(s >= BATCH)
-            def _():
-                u = s - BATCH
-                unit(lax.div(u, RINGS), lax.rem(u, RINGS), c)
+            def four(u, carry, c=c):
+                unit(lax.div(u, RINGS) * 4, 4, lax.rem(u, RINGS), (c,), halves)
+                return carry
+
+            lax.fori_loop(first, first + count, four, 0)
 
         for i, k in enumerate((1, 3, 2)):
 
@@ -217,34 +236,30 @@
                     gy_copy(axis, k, 1 if axis == 0 else 3).wait_recv()
                     gf_copy(axis, k).start()
 
+        @pl.when(s == 13)
+        def _():
+            for axis, k in blocks:
+                gy_copy(axis, k, 3 if axis == 0 else 1).wait_recv()
+                gf_copy(axis, k).wait_recv()
+                gd_copy(axis, k).start()
+
         return carry
 
     lax.fori_loop(1, N - 1, ag_step, 0)
+
+    def two(first):
+        def step(r, carry):
+            unit(first, 2, r, (0, 1, 2), whole)
+            return carry
+
+        lax.fori_loop(0, RINGS, step, 0)
+
+    two(12)
     for c in range(SUBS):
         for r in range(RINGS):
             ag_arrived(r, c, N - 1).wait_recv()
             ag_copy(r, c, N - 2).wait_send()
-
-    mine = pl.ds(pl.multiple_of(core * (4 * PR), 4 * PR), 4 * PR)
-
-    def gd_copy(axis, k):
-        return remote(
-            g_hbm.at[axis, k - 1, mine], g_hbm.at[axis, k - 1, mine],
-            gd_send.at[axis, k - 1], gd_recv.at[axis, k - 1], sibling,
-        )
-
-    blocks = [(axis, k) for axis in range(2) for k in (1, 2, 3)]
-    for axis, k in blocks:
-        gy_copy(axis, k, 3 if axis == 0 else 1).wait_recv()
-        gf_copy(axis, k).wait_recv()
-        gd_copy(axis, k).start()
-
-    def tail(u, carry):
-        for c in range(SUBS):
-            unit(lax.div(u, RINGS), lax.rem(u, RINGS), c)
-        return carry
-
-    lax.fori_loop(N - 1 - BATCH, N, tail, 0)
+    two(14)
 
     def to_bf16(i, carry):
         rows = pl.ds(pl.multiple_of(i * 64, 64), 64)
@@ -253,21 +268,8 @@
 
     lax.fori_loop(0, LEN // 64, to_bf16, 0)
 
-    half = SLOTS * PAGE // 2
-    old_copies = [
-        pltpu.make_async_copy(
-            old_hbm.at[i, pl.ds(p * half, half)], ag.at[p, i, pl.ds(0, half), pl.ds(0, F)], kv_sem.at[p, i]
-        )
-        for p in range(2) for i in range(2)
-    ]
-    kv_copies = [
-        pltpu.make_async_copy(
-            ag.at[p, i, pl.ds(0, half), pl.ds(0, F)], kv_hbm.at[i, pl.ds(p * half, half)], kv_sem.at[p, i]
-        )
-        for p in range(2) for i in range(2)
-    ]
-    for copy in old_copies:
-        copy.start()
+    kv_copy = pltpu.make_async_copy(qkv.at[:, pl.ds(F, 2 * F)], kv_hbm, kv_sem)
+    kv_copy.start()
 
     def home_of(n):
         if n < 8:
@@ -291,37 +293,54 @@
 
     last = len_ref[0] - 1
 
-    def at_copy(axis, h, j):
-        cols = pl.ds(pl.multiple_of(h * HD, HD), HD)
+    def az_copy(h, qi, k):
+        src = att.at[qi, :, :, pl.ds(pl.multiple_of(h * HD, HD), HD)]
+        there = pl.ds(pl.multiple_of(k * F + h * HD, HD), HD)
+        return remote(
+            src, gat.at[1, :, :, there], at_send.at[h, k - 1], at_recv.at[h, k - 1], {"tp": qi * 4 + x}
+        )
+
+    def ax_copy(h, qi, j):
+        src = att.at[qi, lax.rem(x + j, 4), :, pl.ds(pl.multiple_of(h * HD, HD), HD)]
         there = pl.ds(pl.multiple_of((4 - j) * F + h * HD, HD), HD)
-        if axis == 0:
-            src = att.at[:, lax.rem(x + j, 4), :, cols]
-        else:
-            src = att.at[lax.rem(z + j, 4), :, :, cols]
-        return remote(
-            src, gat.at[axis, :, :, there], at_send.at[axis, h, j - 1], at_recv.at[axis, h, 3 - j],
-            along(axis, j),
+        return remote(
+            src, gat.at[0, qi, :, there], ax_send.at[h, qi, j - 1], ax_recv.at[h, qi, 3 - j], along(0, j)
         )
 
     def head(h, carry):
         col = pl.multiple_of(h * HD, HD)
         for qi in range(LEN // BQ):
             kv = -(-(qi + 1) * BQ // HD) * HD
+            free = min(qi * BQ // HD * HD, LEN // 2)
             q = qkv[qi * BQ : (qi + 1) * BQ, pl.ds(col, HD)]
-            k = qkv[0:kv, pl.ds(F + col, HD)]
-            v = qkv[0:kv, pl.ds(2 * F + col, HD)]
-            sc = lax.dot_general(q, k, (((1,), (1,)), ((), ())), preferred_element_type=jnp.float32)
             limit = jnp.minimum(lax.broadcasted_iota(jnp.int32, (BQ, 1), 0) + qi * BQ, last)
-            sc = jnp.where(lax.broadcasted_iota(jnp.int32, (BQ, kv), 1) <= limit, sc, -1e30)
-            top = jnp.max(sc, axis=-1, keepdims=True)
-            e = jnp.exp2((sc - top) * SCALE2)
-            inv = 1.0 / jnp.sum(e, axis=-1, keepdims=True)
-            p = (e * inv).astype(jnp.bfloat16)
-            o = jnp.dot(p, v, preferred_element_type=jnp.float32)
+            parts = []
+            for lo, hi in ((0, free), (free, kv)):
+                if hi > lo:
+                    k = qkv[lo:hi, pl.ds(F + col, HD)]
+                    sc = lax.dot_general(q, k, (((1,), (1,)), ((), ())), preferred_element_type=jnp.float32)
+                    if lo == free:
+                        sc = jnp.where(lax.broadcasted_iota(jnp.int32, (BQ, hi - lo), 1) + lo <= limit, sc, -1e30)
+                    parts.append((lo, hi, sc))
+            top = functools.reduce(jnp.maximum, [jnp.max(sc, axis=-1, keepdims=True) for _, _, sc in parts])
+            parts = [(lo, hi, jnp.exp2((sc - top) * SCALE2)) for lo, hi, sc in parts]
+            inv = 1.0 / sum(jnp.sum(e, axis=-1, keepdims=True) for _, _, e in parts)
+            o = sum(
+                jnp.dot(
+                    (e * inv).astype(jnp.bfloat16),
+                    qkv[lo:hi, pl.ds(2 * F + col, HD)],
+                    preferred_element_type=jnp.float32,
+                )
+                for lo, hi, e in parts
+            )
             att[qi, :, :, pl.ds(col, HD)] = o.astype(jnp.bfloat16).reshape(4, ROWS, HD)
-        for j in (2, 1, 3):
-            for axis in range(2):
-                at_copy(axis, h, j).start()
+            for j in (2, 1, 3):
+                ax_copy(h, qi, j).start()
+
+            @pl.when(z != qi)
+            def _():
+                az_copy(h, qi, lax.rem(z - qi + 4, 4)).start()
+
         return carry
 
     lax.fori_loop(0, HEADS, head, 0)
@@ -329,32 +348,16 @@
         gat[0, b, :, 0:F] = att[b, x]
         gat[1, b, :, 0:F] = att[z, b]
 
-    for copy in old_copies:
-        copy.wait()
-
-    def merge_slot(i, carry):
-        plane, rows = lax.div(i, 6), pl.ds(pl.multiple_of(lax.rem(i, 6) * PAGE, PAGE), PAGE)
-        row = lax.broadcasted_iota(jnp.int32, (PAGE, F), 0)
-        for c in range(2):
-            merged = ag[plane, c, rows, 0:F]
-            for p in range(PAGES):
-                here = (jnp.full((PAGE, F), page_ref[0, p], jnp.int32) == i) & (row + p * PAGE <= last)
-                merged = jnp.where(here, qkv[p * PAGE : (p + 1) * PAGE, (1 + c) * F : (2 + c) * F], merged)
-            ag[plane, c, rows, 0:F] = merged
-        return carry
-
-    lax.fori_loop(0, SLOTS, merge_slot, 0)
     for h in range(HEADS):
-        for j in (1, 2, 3):
-            for axis in range(2):
-                at_copy(axis, h, j).wait_recv()
-    for copy in kv_copies:
-        copy.start()
+        for k in (1, 2, 3):
+            az_copy(h, 0, k).wait_recv()
+            for qi in range(LEN // BQ):
+                ax_copy(h, qi, k).wait_recv()
 
     def p_copy(n, what):
         axis, ahead = 1 - n % 2, (1 if (n // 2) % 2 == 0 else 3)
         here = x if axis == 0 else z
-        j = 4 - ahead if what == 2 else ahead
+        j = (2 if n >= DIRECT else ahead, ahead, 4 - ahead)[what]
         block = lax.rem(here + (2 if what == 0 else j), 4)
         return remote(
             psend.at[n, block], prec.at[n, what], p_send.at[n, what], p_recv.at[n, what], along(axis, j)
@@ -375,11 +378,12 @@
         a = gat[n % 2].reshape(4 * ROWS, KX)
         res = jnp.dot(a, ref[row : row + KX, col : col + CW], preferred_element_type=jnp.float32)
         psend[n] = res.astype(jnp.bfloat16).reshape(4, ROWS, CW)
-        p_copy(n, 0).start()
-        p_copy(n, 2).start()
-        if n >= LAG:
+        for what in range(3):
+            if n >= DIRECT or what != 1:
+                p_copy(n, what).start()
+        if 0 <= n - LAG < DIRECT:
             p_add(n - LAG)
-    for n in range(CHUNKS - LAG, CHUNKS):
+    for n in range(CHUNKS - LAG, DIRECT):
         p_add(n)
 
     for n in range(CHUNKS):
@@ -390,6 +394,9 @@
         total += prec[n, 2].astype(jnp.float32)
         p_copy(n, 1).wait_recv()
         total += prec[n, 1].astype(jnp.float32)
+        if n >= DIRECT:
+            p_copy(n, 0).wait_recv()
+            total += prec[n, 0].astype(jnp.float32)
         out_ref[:, lo : lo + CW] = total.astype(jnp.bfloat16)
 
     for n in range(CHUNKS):
@@ -404,10 +411,54 @@
             gy_copy(axis, k, 3).wait_send()
             gf_copy(axis, k).wait_send()
             gd_copy(axis, k).wait_send()
-        for h in range(HEADS):
-            for j in (1, 2, 3):
-                at_copy(axis, h, j).wait_send()
-    for copy in kv_copies:
+    for h in range(HEADS):
+        for k in (1, 2, 3):
+            az_copy(h, 0, k).wait_send()
+            for qi in range(LEN // BQ):
+                ax_copy(h, qi, k).wait_send()
+    kv_copy.wait()
+
+
+def finish_kernel(page_ref, len_ref, part_hbm, new_hbm, old_hbm, out_hbm, kv_hbm, part, new, kv, in_sem, out_sem):
+    group = SLOTS * PAGE // 4
+    news = [
+        pltpu.make_async_copy(new_hbm.at[pl.ds(g * BQ, BQ)], new.at[pl.ds(g * BQ, BQ)], in_sem.at[g])
+        for g in range(4)
+    ]
+    olds = [
+        pltpu.make_async_copy(
+            old_hbm.at[:, pl.ds(g * group, group)], kv.at[:, pl.ds(g * group, group)], in_sem.at[4 + g]
+        )
+        for g in range(4)
+    ]
+    kvs = [
+        pltpu.make_async_copy(
+            kv.at[:, pl.ds(g * group, group)], kv_hbm.at[:, pl.ds(g * group, group)], out_sem.at[g]
+        )
+        for g in range(4)
+    ]
+    load = pltpu.make_async_copy(part_hbm, part, in_sem.at[8])
+    store = pltpu.make_async_copy(part, out_hbm, out_sem.at[4])
+    for copy in [*news, *olds, load]:
+        copy.start()
+    for copy in news:
+        copy.wait()
+    for g in range(4):
+        olds[g].wait()
+        for i in range(g * SLOTS // 4, (g + 1) * SLOTS // 4):
+            page = jnp.int32(-1)
+            for p in range(PAGES):
+                page = jnp.where(page_ref[0, p] == i, p, page)
+            row = lax.broadcasted_iota(jnp.int32, (PAGE, 1), 0) + page * PAGE
+            written = (row < len_ref[0]) & (row >= 0)
+            rows = pl.ds(pl.multiple_of(jnp.maximum(page, 0) * PAGE, PAGE), PAGE)
+            for c in range(2):
+                old = kv[c, i * PAGE : (i + 1) * PAGE, :]
+                kv[c, i * PAGE : (i + 1) * PAGE, :] = jnp.where(written, new[rows, c * F : (c + 1) * F], old)
+        kvs[g].start()
+    load.wait()
+    store.start()
+    for copy in [*kvs, store]:
         copy.wait()
 
 
@@ -416,14 +467,14 @@
     anym = pl.BlockSpec(memory_space=pl.ANY)
     smem = pl.BlockSpec(memory_space=pltpu.SMEM)
     dma = pltpu.SemaphoreType.DMA
-    out, kv_out, _ = pl.pallas_call(
+    part, kv_new, _ = pl.pallas_call(
         main_kernel,
         out_shape=(
             jax.ShapeDtypeStruct((ROWS, D), jnp.bfloat16),
-            jax.ShapeDtypeStruct((2, SLOTS * PAGE, F), jnp.bfloat16),
+            jax.ShapeDtypeStruct((LEN, 2 * F), jnp.bfloat16),
             jax.ShapeDtypeStruct((2, 3, F, HC), jnp.bfloat16),
         ),
-        in_specs=[smem, smem, vmem, vmem, vmem, anym, vmem, anym, vmem, anym],
+        in_specs=[smem, vmem, vmem, vmem, anym, vmem, anym, vmem],
         out_specs=(vmem, anym, anym),
         scratch_shapes=[
             pltpu.VMEM((RINGS, SUBS, LEN, CW), jnp.bfloat16),
@@ -438,7 +489,7 @@
             dma((RINGS, SUBS)),
             dma((RINGS, SUBS, N)),
             dma((3,)),
-            dma((2, 2)),
+            dma,
             dma((2, 3)),
             dma((2, 3)),
             dma((2, 3)),
@@ -450,8 +501,10 @@
             dma((2, 3)),
             dma((2, 3)),
             dma((CHUNKS, 4)),
-            dma((2, HEADS, 3)),
-            dma((2, HEADS, 3)),
+            dma((HEADS, 3)),
+            dma((HEADS, 3)),
+            dma((HEADS, 4, 3)),
+            dma((HEADS, 4, 3)),
             dma((CHUNKS, 3)),
             dma((CHUNKS, 3)),
         ],
@@ -461,7 +514,6 @@
         name="sublayer",
     )(
         lengths,
-        page_table,
         tokens,
         ln_gain.reshape(1, D),
         ln_bias.reshape(1, D),
@@ -469,8 +521,24 @@
         b_qkv,
         w_out,
         b_out.reshape(1, D),
-        kv_cache.reshape(2, SLOTS * PAGE, F),
     )
+    out, kv_out = pl.pallas_call(
+        finish_kernel,
+        out_shape=(
+            jax.ShapeDtypeStruct((ROWS, D), jnp.bfloat16),
+            jax.ShapeDtypeStruct((2, SLOTS * PAGE, F), jnp.bfloat16),
+        ),
+        in_specs=[smem, smem, anym, anym, anym],
+        out_specs=(anym, anym),
+        scratch_shapes=[
+            pltpu.VMEM((ROWS, D), jnp.bfloat16),
+            pltpu.VMEM((LEN, 2 * F), jnp.bfloat16),
+            pltpu.VMEM((2, SLOTS * PAGE, F), jnp.bfloat16),
+            dma((9,)),
+            dma((5,)),
+        ],
+        name="finish",
+    )(page_table, lengths, part, kv_new, kv_cache.reshape(2, SLOTS * PAGE, F))
     return out, kv_out.reshape(kv_cache.shape)
 
 

time: 159 us -> 153 us (0.962)
  local copies, waits for them, and re-layouts: 5.63 us -> 0 us
    unnamed x2 -> x0, local copies, waits for them, and re-layouts: 5.63 us -> none
    pallas_call x1, Pallas kernels: 151 us -> 147 us  [body(): pl.pallas_call(main_kernel, out_shape=(jax.ShapeDtypeStruct((ROWS, D), jn...]
    pallas_call x0 -> x1, Pallas kernels: none -> 4.27 us  [body(): pl.pallas_call(finish_kernel, out_shape=(jax.ShapeDtypeStruct((ROWS, D),...]
where the time goes in v3:
time: 153 us; the launch traced here: 152 us
  Pallas kernels  151 us (99%)
    pallas_call x1, Pallas kernels, body(): pl.pallas_call(main_kernel, out_shape=(jax.ShapeDtypeStruct((ROWS, D), jn...  147 us
    pallas_call x1, Pallas kernels, body(): pl.pallas_call(finish_kernel, out_shape=(jax.ShapeDtypeStruct((ROWS, D),...  4.27 us

profile of v3, /device:TPU:0, one launch (start us, length us, event | category | flops | bytes accessed | tf_op | source)
XLA Modules:
  0.0 152.4 jit_solution(8434258319661980857)
XLA Ops:
  1.3 146.7 %sublayer.1 = (bf16[80,6144]{1,0:T(8,128)(2,1)}, bf16[1280,768]{1,0:T(8,128)(2,1)}, bf16[2,3,384,3072]{3,2,1,0:T(8,128)(2,1)}) custom-call(s32[1]{0:T(128)S(6)} %copy.12.len_ref, bf16[80,6144]{1,0:T(8,128)(2,1)} %tok_ref.1, f32[1,6144]{1,0:T(1,128)} %bitcast.8, f32[1,6144]{1,0:T(1,128)} %bitcast.9, bf16[3,6144,384]{2,1,0:T(8,128)(2,1)} %bitcast.6, ...), custom_call_target="tpu_custom_call" | custom-call | tf_op jit(solution)/shard_map/sublayer/pallas_call | solution.py:470
  147.9 4.3 %finish.1 = (bf16[80,6144]{1,0:T(8,128)(2,1)}, bf16[2,1536,384]{2,1,0:T(8,128)(2,1)}) custom-call(s32[1,10]{1,0:T(1,128)} %page_ref.1, s32[1]{0:T(128)S(6)} %copy.12.len_ref, bf16[80,6144]{1,0:T(8,128)(2,1)} %get-tuple-element.6.part_hbm, bf16[1280,768]{1,0:T(8,128)(2,1)} %get-tuple-element.7.new_hbm, bf16[2,1536,384]{2,1,0:T(8,128)(2,1)} %bitcast.7), custom_call_target="tpu_custom_call" | custom-call | tf_op jit(solution)/shard_map/finish/pallas_call | solution.py:525

commit v4 on v3

--- a/solution.py
+++ b/solution.py
@@ -30,7 +30,8 @@
 KX = 4 * F
 CHUNKS = 12
 LAG = 4
-DIRECT = 8
+RC = 160
+SPAN = 4
 FORWARD_AT = 4
 SCALE2 = 1.4426950408889634 / (HD ** 0.5)
 
@@ -54,10 +55,10 @@
 def main_kernel(
     len_ref, tok_ref, gain_ref, shift_ref, w_hbm, bq_ref, wo_hbm, bo_ref,
     out_ref, kv_hbm, g_hbm,
-    ag, w, acc, qkv, att, wx, gat, psend, prec,
-    ag_send, ag_recv, w_sem, kv_sem,
-    g1_send, g1_recv, g2_send, g2_recv, gy_send, gy_recv, gf_send, gf_recv, gd_send, gd_recv,
-    l_sem, at_send, at_recv, ax_send, ax_recv, p_send, p_recv,
+    ag, w, acc, qkv, att, wx, gat, psend, prec, sbuf, out,
+    ag_send, ag_recv, w_sem, kv_sem, out_sem,
+    g_send, g1_recv, g2_recv, gy_recv, gf_recv, gd_recv,
+    l_sem, az_send, az_recv, ax_send, ax_recv, p_send, p0_recv, p_recv,
 ):
     tp = lax.axis_index("tp")
     dp = lax.axis_index("dp")
@@ -84,7 +85,7 @@
         pl.semaphore_signal(barrier, inc=1, device_id=peer, device_id_type=MESH)
 
     w_copies = [
-        pltpu.make_async_copy(w_hbm.at[c], w.at[:, pl.ds(c * F, F)], w_sem.at[c]) for c in range(3)
+        pltpu.make_async_copy(w_hbm.at[c], w.at[:, pl.ds(c * F, F)], w_sem) for c in range(3)
     ]
     for copy in w_copies:
         copy.start()
@@ -101,7 +102,7 @@
     def g1_copy(axis, j):
         return remote(
             wo_hbm.at[piece, pl.ds(axis * HC, HC)], g_hbm.at[axis, 3 - j, piece],
-            g1_send.at[axis, 3 - j], g1_recv.at[axis, 3 - j], along(axis, j),
+            g_send.at[0], g1_recv.at[axis, j // 2], along(axis, j),
         )
 
     def g2_copy(axis, j):
@@ -109,7 +110,7 @@
         cols = pl.ds(0 if j == 1 else HC // 2, HC // 2)
         return remote(
             g_hbm.at[axis, k - 1, piece, cols], g_hbm.at[axis, 1, piece, cols],
-            g2_send.at[axis, 3 - j], g2_recv.at[axis, 3 - j], along(axis, j),
+            g_send.at[1], g2_recv.at[axis, j // 2], along(axis, j),
         )
 
     for axis in range(2):
@@ -138,13 +139,13 @@
     def ag_copy(r, c, s):
         return remote(
             ag.at[r, c, slot(s)], ag.at[r, c, slot(s + 1)],
-            ag_send.at[r, c], ag_recv.at[r, c, s + 1], {"tp": nxt[r]},
+            ag_send.at[r, c], ag_recv.at[r, c, lax.rem(s + 1, SPAN)], {"tp": nxt[r]},
         )
 
     def ag_arrived(r, c, s):
         return remote(
             ag.at[r, c, slot(s)], ag.at[r, c, slot(s)],
-            ag_send.at[r, c], ag_recv.at[r, c, s], {"tp": nxt[r]},
+            ag_send.at[r, c], ag_recv.at[r, c, lax.rem(s, SPAN)], {"tp": nxt[r]},
         )
 
     for r in range(RINGS):
@@ -159,13 +160,12 @@
 
     for c in range(3):
         acc[:, c * F : (c + 1) * F] = jnp.broadcast_to(bq_ref[c : c + 1, :], (LEN, F))
-    for copy in w_copies:
-        copy.wait()
+    pltpu.make_async_copy(w, w, w_sem).wait()
 
     def gy_copy(axis, k, j):
         return remote(
             g_hbm.at[axis, k - 1, piece], g_hbm.at[axis, k - 1, piece],
-            gy_send.at[axis, k - 1, j // 2], gy_recv.at[axis, k - 1, j // 2], along_y(j),
+            g_send.at[2 + axis], gy_recv.at[axis, k - 1, j // 2], along_y(j),
         )
 
     def gf_copy(axis, k):
@@ -173,7 +173,7 @@
         src = pl.ds(pl.multiple_of((core * 4 + lax.rem(y + 4 - j, 4)) * PR, PR), PR)
         return remote(
             g_hbm.at[axis, k - 1, src], g_hbm.at[axis, k - 1, src],
-            gf_send.at[axis, k - 1], gf_recv.at[axis, k - 1], along_y(j),
+            g_send.at[4], gf_recv.at[axis, k - 1], along_y(j),
         )
 
     for k in (1, 3, 2):
@@ -208,7 +208,7 @@
     def gd_copy(axis, k):
         return remote(
             g_hbm.at[axis, k - 1, mine], g_hbm.at[axis, k - 1, mine],
-            gd_send.at[axis, k - 1], gd_recv.at[axis, k - 1], sibling,
+            g_send.at[5], gd_recv.at[axis, k - 1], sibling,
         )
 
     blocks = [(axis, k) for axis in range(2) for k in (1, 2, 3)]
@@ -283,13 +283,12 @@
             src = wo_hbm.at[:, pl.ds(axis * HC + m * CW, CW)]
         else:
             src = g_hbm.at[axis, k - 1, :, pl.ds(m * CW, CW)]
-        return pltpu.make_async_copy(src, ref.at[pl.ds(row + k * F, F), pl.ds(col, CW)], l_sem.at[n, k])
-
-    for axis, k in blocks:
-        gd_copy(axis, k).wait_recv()
-    for n in range(CHUNKS):
-        for k in range(4):
-            load(n, k).start()
+        return pltpu.make_async_copy(src, ref.at[pl.ds(row + k * F, F), pl.ds(col, CW)], l_sem.at[n])
+
+    def loaded(n):
+        ref, row, col = home_of(n)
+        chunk = ref.at[pl.ds(row, KX), pl.ds(col, CW)]
+        return pltpu.make_async_copy(chunk, chunk, l_sem.at[n])
 
     last = len_ref[0] - 1
 
@@ -297,49 +296,64 @@
         src = att.at[qi, :, :, pl.ds(pl.multiple_of(h * HD, HD), HD)]
         there = pl.ds(pl.multiple_of(k * F + h * HD, HD), HD)
         return remote(
-            src, gat.at[1, :, :, there], at_send.at[h, k - 1], at_recv.at[h, k - 1], {"tp": qi * 4 + x}
+            src, gat.at[1, :, :, there], az_send.at[h, k - 1], az_recv.at[h, k - 1], {"tp": qi * 4 + x}
         )
 
     def ax_copy(h, qi, j):
         src = att.at[qi, lax.rem(x + j, 4), :, pl.ds(pl.multiple_of(h * HD, HD), HD)]
         there = pl.ds(pl.multiple_of((4 - j) * F + h * HD, HD), HD)
         return remote(
-            src, gat.at[0, qi, :, there], ax_send.at[h, qi, j - 1], ax_recv.at[h, qi, 3 - j], along(0, j)
-        )
+            src, gat.at[0, qi, :, there], ax_send.at[h, j - 1], ax_recv.at[h, 3 - j], along(0, j)
+        )
+
+    def ax_all(h, k):
+        part = gat.at[0, :, :, pl.ds(h * HD, HD)]
+        return remote(part, part, ax_send.at[h, k - 1], ax_recv.at[h, k - 1], along(0, k))
 
     def head(h, carry):
         col = pl.multiple_of(h * HD, HD)
         for qi in range(LEN // BQ):
-            kv = -(-(qi + 1) * BQ // HD) * HD
-            free = min(qi * BQ // HD * HD, LEN // 2)
-            q = qkv[qi * BQ : (qi + 1) * BQ, pl.ds(col, HD)]
-            limit = jnp.minimum(lax.broadcasted_iota(jnp.int32, (BQ, 1), 0) + qi * BQ, last)
-            parts = []
-            for lo, hi in ((0, free), (free, kv)):
-                if hi > lo:
+            for half in range(BQ // RC):
+                top_row = qi * BQ + half * RC
+                kv = -(-(top_row + RC) // HD) * HD
+                q = qkv[top_row : top_row + RC, pl.ds(col, HD)]
+                limit = jnp.minimum(lax.broadcasted_iota(jnp.int32, (RC, 1), 0) + top_row, last)
+                tiles = [(lo, min(lo + 256, kv)) for lo in range(0, kv, 256)]
+                most = None
+                for lo, hi in tiles:
                     k = qkv[lo:hi, pl.ds(F + col, HD)]
                     sc = lax.dot_general(q, k, (((1,), (1,)), ((), ())), preferred_element_type=jnp.float32)
-                    if lo == free:
-                        sc = jnp.where(lax.broadcasted_iota(jnp.int32, (BQ, hi - lo), 1) + lo <= limit, sc, -1e30)
-                    parts.append((lo, hi, sc))
-            top = functools.reduce(jnp.maximum, [jnp.max(sc, axis=-1, keepdims=True) for _, _, sc in parts])
-            parts = [(lo, hi, jnp.exp2((sc - top) * SCALE2)) for lo, hi, sc in parts]
-            inv = 1.0 / sum(jnp.sum(e, axis=-1, keepdims=True) for _, _, e in parts)
-            o = sum(
-                jnp.dot(
-                    (e * inv).astype(jnp.bfloat16),
-                    qkv[lo:hi, pl.ds(2 * F + col, HD)],
-                    preferred_element_type=jnp.float32,
-                )
-                for lo, hi, e in parts
-            )
-            att[qi, :, :, pl.ds(col, HD)] = o.astype(jnp.bfloat16).reshape(4, ROWS, HD)
+                    if hi > min(top_row + 1, LEN // 2 + 1):
+                        sc = jnp.where(lax.broadcasted_iota(jnp.int32, (RC, hi - lo), 1) + lo <= limit, sc, -1e30)
+                    sbuf[:, lo:hi] = sc
+                    for t in range(0, hi - lo, HD):
+                        most = sc[:, t : t + HD] if most is None else jnp.maximum(most, sc[:, t : t + HD])
+                top = jnp.max(most, axis=-1, keepdims=True) * SCALE2
+                total = None
+                for t in range(0, kv, HD):
+                    e = jnp.exp2(sbuf[:, t : t + HD] * SCALE2 - top)
+                    total = e if total is None else total + e
+                top = top + jnp.log2(jnp.sum(total, axis=-1, keepdims=True))
+                o = None
+                for lo, hi in tiles:
+                    p = jnp.exp2(sbuf[:, lo:hi] * SCALE2 - top).astype(jnp.bfloat16)
+                    part = jnp.dot(p, qkv[lo:hi, pl.ds(2 * F + col, HD)], preferred_element_type=jnp.float32)
+                    o = part if o is None else o + part
+                att[qi, 2 * half : 2 * half + 2, :, pl.ds(col, HD)] = o.astype(jnp.bfloat16).reshape(2, ROWS, HD)
             for j in (2, 1, 3):
                 ax_copy(h, qi, j).start()
 
             @pl.when(z != qi)
             def _():
                 az_copy(h, qi, lax.rem(z - qi + 4, 4)).start()
+
+        @pl.when(h == 0)
+        def _():
+            for axis, k in blocks:
+                gd_copy(axis, k).wait_recv()
+            for n in range(CHUNKS):
+                for k in range(4):
+                    load(n, k).start()
 
         return carry
 
@@ -351,17 +365,25 @@
     for h in range(HEADS):
         for k in (1, 2, 3):
             az_copy(h, 0, k).wait_recv()
-            for qi in range(LEN // BQ):
-                ax_copy(h, qi, k).wait_recv()
+            ax_all(h, k).wait_recv()
+
+    def out_copy(n):
+        lo = (n % 2) * HC + (n // 2) * CW
+        return pltpu.make_async_copy(out.at[n], out_ref.at[:, pl.ds(lo, CW)], out_sem.at[n])
 
     def p_copy(n, what):
         axis, ahead = 1 - n % 2, (1 if (n // 2) % 2 == 0 else 3)
         here = x if axis == 0 else z
-        j = (2 if n >= DIRECT else ahead, ahead, 4 - ahead)[what]
+        j = (ahead, ahead, 4 - ahead)[what]
         block = lax.rem(here + (2 if what == 0 else j), 4)
         return remote(
-            psend.at[n, block], prec.at[n, what], p_send.at[n, what], p_recv.at[n, what], along(axis, j)
-        )
+            psend.at[n, block], prec.at[n, what], p_send.at[n],
+            p0_recv.at[n] if what == 0 else p_recv.at[n], along(axis, j),
+        )
+
+    def p_all(n, count):
+        part = prec.at[n, pl.ds(0, count)]
+        return remote(part, part, p_send.at[n], p_recv.at[n], along(0, 1))
 
     def p_add(n):
         axis, ahead = 1 - n % 2, (1 if (n // 2) % 2 == 0 else 3)
@@ -373,49 +395,45 @@
 
     for n in range(CHUNKS):
         ref, row, col = home_of(n)
-        for k in range(4):
-            load(n, k).wait()
+        loaded(n).wait()
         a = gat[n % 2].reshape(4 * ROWS, KX)
         res = jnp.dot(a, ref[row : row + KX, col : col + CW], preferred_element_type=jnp.float32)
         psend[n] = res.astype(jnp.bfloat16).reshape(4, ROWS, CW)
-        for what in range(3):
-            if n >= DIRECT or what != 1:
-                p_copy(n, what).start()
-        if 0 <= n - LAG < DIRECT:
+        p_copy(n, 0).start()
+        p_copy(n, 2).start()
+        if n >= LAG:
             p_add(n - LAG)
-    for n in range(CHUNKS - LAG, DIRECT):
+    for n in range(CHUNKS - LAG, CHUNKS):
         p_add(n)
 
     for n in range(CHUNKS):
         here = z if n % 2 == 0 else x
         lo = (n % 2) * HC + (n // 2) * CW
         total = psend[n, here].astype(jnp.float32) + bo_ref[:, lo : lo + CW]
-        p_copy(n, 2).wait_recv()
-        total += prec[n, 2].astype(jnp.float32)
-        p_copy(n, 1).wait_recv()
-        total += prec[n, 1].astype(jnp.float32)
-        if n >= DIRECT:
-            p_copy(n, 0).wait_recv()
-            total += prec[n, 0].astype(jnp.float32)
-        out_ref[:, lo : lo + CW] = total.astype(jnp.bfloat16)
+        p_all(n, 2).wait_recv()
+        total += prec[n, 1].astype(jnp.float32) + prec[n, 2].astype(jnp.float32)
+        out[n] = total.astype(jnp.bfloat16)
+        out_copy(n).start()
 
     for n in range(CHUNKS):
-        for what in range(3):
-            p_copy(n, what).wait_send()
-    for axis in range(2):
-        for j in (1, 3):
-            g1_copy(axis, j).wait_send()
-            g2_copy(axis, j).wait_send()
-        for k in (1, 2, 3):
-            gy_copy(axis, k, 1).wait_send()
-            gy_copy(axis, k, 3).wait_send()
-            gf_copy(axis, k).wait_send()
-            gd_copy(axis, k).wait_send()
+        p_all(n, 3).wait_send()
+    for i, sent in enumerate(
+        (
+            g_hbm.at[0, 0, pl.ds(0, 4 * PR)],
+            g_hbm.at[0, 0, pl.ds(0, 2 * PR)],
+            g_hbm.at[0, 0, pl.ds(0, 6 * PR)],
+            g_hbm.at[0, 0, pl.ds(0, 6 * PR)],
+            g_hbm.at[0, 0, pl.ds(0, 6 * PR)],
+            g_hbm.at[0],
+        )
+    ):
+        remote(sent, sent, g_send.at[i], gd_recv.at[0, 0], sibling).wait_send()
     for h in range(HEADS):
         for k in (1, 2, 3):
             az_copy(h, 0, k).wait_send()
-            for qi in range(LEN // BQ):
-                ax_copy(h, qi, k).wait_send()
+            ax_all(h, k).wait_send()
+    for n in range(CHUNKS):
+        out_copy(n).wait()
     kv_copy.wait()
 
 
@@ -475,7 +493,7 @@
             jax.ShapeDtypeStruct((2, 3, F, HC), jnp.bfloat16),
         ),
         in_specs=[smem, vmem, vmem, vmem, anym, vmem, anym, vmem],
-        out_specs=(vmem, anym, anym),
+        out_specs=(anym, anym, anym),
         scratch_shapes=[
             pltpu.VMEM((RINGS, SUBS, LEN, CW), jnp.bfloat16),
             pltpu.VMEM((D, 3 * F), jnp.bfloat16),
@@ -486,27 +504,27 @@
             pltpu.VMEM((2, 4, ROWS, KX), jnp.bfloat16),
             pltpu.VMEM((CHUNKS, 4, ROWS, CW), jnp.bfloat16),
             pltpu.VMEM((CHUNKS, 3, ROWS, CW), jnp.bfloat16),
+            pltpu.VMEM((RC, LEN), jnp.float32),
+            pltpu.VMEM((CHUNKS, ROWS, CW), jnp.bfloat16),
             dma((RINGS, SUBS)),
-            dma((RINGS, SUBS, N)),
-            dma((3,)),
+            dma((RINGS, SUBS, SPAN)),
             dma,
-            dma((2, 3)),
-            dma((2, 3)),
-            dma((2, 3)),
-            dma((2, 3)),
-            dma((2, 3, 2)),
+            dma,
+            dma((CHUNKS,)),
+            dma((6,)),
+            dma((2, 2)),
+            dma((2, 2)),
             dma((2, 3, 2)),
             dma((2, 3)),
             dma((2, 3)),
-            dma((2, 3)),
-            dma((2, 3)),
-            dma((CHUNKS, 4)),
+            dma((CHUNKS,)),
             dma((HEADS, 3)),
             dma((HEADS, 3)),
-            dma((HEADS, 4, 3)),
-            dma((HEADS, 4, 3)),
-            dma((CHUNKS, 3)),
-            dma((CHUNKS, 3)),
+            dma((HEADS, 3)),
+            dma((HEADS, 3)),
+            dma((CHUNKS,)),
+            dma((CHUNKS,)),
+            dma((CHUNKS,)),
         ],
         compiler_params=pltpu.CompilerParams(
             collective_id=0, has_side_effects=True, vmem_limit_bytes=67043328

time: 153 us -> 149 us (0.974)
  Pallas kernels: 151 us -> 147 us
    pallas_call x1, Pallas kernels: 147 us -> 143 us  [body(): pl.pallas_call(main_kernel, out_shape=(jax.ShapeDtypeStruct((ROWS, D), jn...]
where the time goes in v4:
time: 149 us; the launch traced here: 148 us
  Pallas kernels  147 us (99%)
    pallas_call x1, Pallas kernels, body(): pl.pallas_call(main_kernel, out_shape=(jax.ShapeDtypeStruct((ROWS, D), jn...  143 us
    pallas_call x1, Pallas kernels, body(): pl.pallas_call(finish_kernel, out_shape=(jax.ShapeDtypeStruct((ROWS, D),...  4.27 us

profile of v4, /device:TPU:0, one launch (start us, length us, event | category | flops | bytes accessed | tf_op | source)
XLA Modules:
  0.0 148.5 jit_solution(15234277074758015013)
XLA Ops:
  1.3 142.7 %sublayer.1 = (bf16[80,6144]{1,0:T(8,128)(2,1)}, bf16[1280,768]{1,0:T(8,128)(2,1)}, bf16[2,3,384,3072]{3,2,1,0:T(8,128)(2,1)}) custom-call(s32[1]{0:T(128)S(6)} %copy.12.len_ref, bf16[80,6144]{1,0:T(8,128)(2,1)} %tok_ref.1, f32[1,6144]{1,0:T(1,128)} %bitcast.8, f32[1,6144]{1,0:T(1,128)} %bitcast.9, bf16[3,6144,384]{2,1,0:T(8,128)(2,1)} %bitcast.6, ...), custom_call_target="tpu_custom_call" | custom-call | tf_op jit(solution)/shard_map/sublayer/pallas_call | solution.py:488
  144.0 4.3 %finish.1 = (bf16[80,6144]{1,0:T(8,128)(2,1)}, bf16[2,1536,384]{2,1,0:T(8,128)(2,1)}) custom-call(s32[1,10]{1,0:T(1,128)} %page_ref.1, s32[1]{0:T(128)S(6)} %copy.12.len_ref, bf16[80,6144]{1,0:T(8,128)(2,1)} %get-tuple-element.6.part_hbm, bf16[1280,768]{1,0:T(8,128)(2,1)} %get-tuple-element.7.new_hbm, bf16[2,1536,384]{2,1,0:T(8,128)(2,1)} %bitcast.7), custom_call_target="tpu_custom_call" | custom-call | tf_op jit(solution)/shard_map/finish/pallas_call | solution.py:543

commit v5 on v4

--- a/solution.py
+++ b/solution.py
@@ -30,7 +30,8 @@
 KX = 4 * F
 CHUNKS = 12
 LAG = 4
-RC = 160
+QB = 128
+PIECES = ((0, 320, 0), (320, 640, 1), (640, 960, 2), (960, 1152, 3), (1152, 1280, 3))
 SPAN = 4
 FORWARD_AT = 4
 SCALE2 = 1.4426950408889634 / (HD ** 0.5)
@@ -55,7 +56,7 @@
 def main_kernel(
     len_ref, tok_ref, gain_ref, shift_ref, w_hbm, bq_ref, wo_hbm, bo_ref,
     out_ref, kv_hbm, g_hbm,
-    ag, w, acc, qkv, att, wx, gat, psend, prec, sbuf, out,
+    ag, w, acc, qkv, att, wx, gat, psend, prec, out,
     ag_send, ag_recv, w_sem, kv_sem, out_sem,
     g_send, g1_recv, g2_recv, gy_recv, gf_recv, gd_recv,
     l_sem, az_send, az_recv, ax_send, ax_recv, p_send, p0_recv, p_recv,
@@ -292,60 +293,60 @@
 
     last = len_ref[0] - 1
 
-    def az_copy(h, qi, k):
-        src = att.at[qi, :, :, pl.ds(pl.multiple_of(h * HD, HD), HD)]
+    def az_copy(h, lo, hi, qi, k):
+        src = att.at[pl.ds(lo, hi - lo), pl.ds(pl.multiple_of(h * HD, HD), HD)]
         there = pl.ds(pl.multiple_of(k * F + h * HD, HD), HD)
         return remote(
-            src, gat.at[1, :, :, there], az_send.at[h, k - 1], az_recv.at[h, k - 1], {"tp": qi * 4 + x}
+            src, gat.at[1, pl.ds(lo - qi * BQ, hi - lo), there],
+            az_send.at[h], az_recv.at[h, k - 1], {"tp": qi * 4 + x},
         )
 
     def ax_copy(h, qi, j):
-        src = att.at[qi, lax.rem(x + j, 4), :, pl.ds(pl.multiple_of(h * HD, HD), HD)]
+        block = pl.ds(pl.multiple_of((4 * qi + lax.rem(x + j, 4)) * ROWS, 16), ROWS)
+        src = att.at[block, pl.ds(pl.multiple_of(h * HD, HD), HD)]
         there = pl.ds(pl.multiple_of((4 - j) * F + h * HD, HD), HD)
         return remote(
-            src, gat.at[0, qi, :, there], ax_send.at[h, j - 1], ax_recv.at[h, 3 - j], along(0, j)
-        )
-
-    def ax_all(h, k):
-        part = gat.at[0, :, :, pl.ds(h * HD, HD)]
-        return remote(part, part, ax_send.at[h, k - 1], ax_recv.at[h, k - 1], along(0, k))
+            src, gat.at[0, pl.ds(qi * ROWS, ROWS), there], ax_send.at[h], ax_recv.at[h, 3 - j], along(0, j)
+        )
+
+    def a_all(axis, h, k):
+        part = gat.at[axis, :, pl.ds(h * HD, HD)]
+        sends, recvs = ((ax_send, ax_recv), (az_send, az_recv))[axis]
+        return remote(part, part, sends.at[h], recvs.at[h, k - 1], along(axis, k))
+
+    def a_sent(axis, h):
+        part = gat.at[axis, :, pl.ds(0, 3 * HD)]
+        return remote(part, part, (ax_send, az_send)[axis].at[h], ax_recv.at[h, 0], along(0, 1))
 
     def head(h, carry):
         col = pl.multiple_of(h * HD, HD)
-        for qi in range(LEN // BQ):
-            for half in range(BQ // RC):
-                top_row = qi * BQ + half * RC
-                kv = -(-(top_row + RC) // HD) * HD
-                q = qkv[top_row : top_row + RC, pl.ds(col, HD)]
-                limit = jnp.minimum(lax.broadcasted_iota(jnp.int32, (RC, 1), 0) + top_row, last)
-                tiles = [(lo, min(lo + 256, kv)) for lo in range(0, kv, 256)]
-                most = None
-                for lo, hi in tiles:
-                    k = qkv[lo:hi, pl.ds(F + col, HD)]
-                    sc = lax.dot_general(q, k, (((1,), (1,)), ((), ())), preferred_element_type=jnp.float32)
-                    if hi > min(top_row + 1, LEN // 2 + 1):
-                        sc = jnp.where(lax.broadcasted_iota(jnp.int32, (RC, hi - lo), 1) + lo <= limit, sc, -1e30)
-                    sbuf[:, lo:hi] = sc
-                    for t in range(0, hi - lo, HD):
-                        most = sc[:, t : t + HD] if most is None else jnp.maximum(most, sc[:, t : t + HD])
-                top = jnp.max(most, axis=-1, keepdims=True) * SCALE2
-                total = None
-                for t in range(0, kv, HD):
-                    e = jnp.exp2(sbuf[:, t : t + HD] * SCALE2 - top)
-                    total = e if total is None else total + e
-                top = top + jnp.log2(jnp.sum(total, axis=-1, keepdims=True))
-                o = None
-                for lo, hi in tiles:
-                    p = jnp.exp2(sbuf[:, lo:hi] * SCALE2 - top).astype(jnp.bfloat16)
-                    part = jnp.dot(p, qkv[lo:hi, pl.ds(2 * F + col, HD)], preferred_element_type=jnp.float32)
-                    o = part if o is None else o + part
-                att[qi, 2 * half : 2 * half + 2, :, pl.ds(col, HD)] = o.astype(jnp.bfloat16).reshape(2, ROWS, HD)
-            for j in (2, 1, 3):
-                ax_copy(h, qi, j).start()
-
-            @pl.when(z != qi)
-            def _():
-                az_copy(h, qi, lax.rem(z - qi + 4, 4)).start()
+        for row in range(0, LEN, QB):
+            kv = row + QB
+            free = min(row, LEN // 2)
+            q = qkv[row : row + QB, pl.ds(col, HD)]
+            k = qkv[0:kv, pl.ds(F + col, HD)]
+            v = qkv[0:kv, pl.ds(2 * F + col, HD)]
+            sc = lax.dot_general(k, q, (((1,), (1,)), ((), ())), preferred_element_type=jnp.float32)
+            limit = jnp.minimum(lax.broadcasted_iota(jnp.int32, (1, QB), 1) + row, last)
+            key = lax.broadcasted_iota(jnp.int32, (kv - free, QB), 0) + free
+            masked = jnp.where(key <= limit, sc[free:], -1e30)
+            sc = jnp.concatenate([sc[:free], masked], axis=0) if free else masked
+            top = jnp.max(sc, axis=0, keepdims=True)
+            e = jnp.exp2((sc - top) * SCALE2)
+            inv = 1.0 / jnp.sum(e, axis=0, keepdims=True)
+            p = (e * inv).astype(jnp.bfloat16)
+            o = lax.dot_general(p, v, (((0,), (0,)), ((), ())), preferred_element_type=jnp.float32)
+            att[row : row + QB, pl.ds(col, HD)] = o.astype(jnp.bfloat16)
+            for lo, hi, qi in PIECES:
+                if row < hi <= kv:
+
+                    @pl.when(z != qi)
+                    def _():
+                        az_copy(h, lo, hi, qi, lax.rem(z - qi + 4, 4)).start()
+
+                    if hi == (qi + 1) * BQ:
+                        for j in (2, 1, 3):
+                            ax_copy(h, qi, j).start()
 
         @pl.when(h == 0)
         def _():
@@ -359,13 +360,8 @@
 
     lax.fori_loop(0, HEADS, head, 0)
     for b in range(4):
-        gat[0, b, :, 0:F] = att[b, x]
-        gat[1, b, :, 0:F] = att[z, b]
-
-    for h in range(HEADS):
-        for k in (1, 2, 3):
-            az_copy(h, 0, k).wait_recv()
-            ax_all(h, k).wait_recv()
+        gat[0, b * ROWS : (b + 1) * ROWS, 0:F] = att[pl.ds(pl.multiple_of((4 * b + x) * ROWS, 16), ROWS), :]
+    gat[1, :, 0:F] = att[pl.ds(pl.multiple_of(z * BQ, 64), BQ), :]
 
     def out_copy(n):
         lo = (n % 2) * HC + (n // 2) * CW
@@ -395,9 +391,12 @@
 
     for n in range(CHUNKS):
         ref, row, col = home_of(n)
+        if n < 2:
+            for h in range(HEADS):
+                for k in (1, 2, 3):
+                    a_all(n, h, k).wait_recv()
         loaded(n).wait()
-        a = gat[n % 2].reshape(4 * ROWS, KX)
-        res = jnp.dot(a, ref[row : row + KX, col : col + CW], preferred_element_type=jnp.float32)
+        res = jnp.dot(gat[n % 2], ref[row : row + KX, col : col + CW], preferred_element_type=jnp.float32)
         psend[n] = res.astype(jnp.bfloat16).reshape(4, ROWS, CW)
         p_copy(n, 0).start()
         p_copy(n, 2).start()
@@ -429,9 +428,8 @@
     ):
         remote(sent, sent, g_send.at[i], gd_recv.at[0, 0], sibling).wait_send()
     for h in range(HEADS):
-        for k in (1, 2, 3):
-            az_copy(h, 0, k).wait_send()
-            ax_all(h, k).wait_send()
+        for axis in range(2):
+            a_sent(axis, h).wait_send()
     for n in range(CHUNKS):
         out_copy(n).wait()
     kv_copy.wait()
@@ -499,12 +497,11 @@
             pltpu.VMEM((D, 3 * F), jnp.bfloat16),
             pltpu.VMEM((LEN, 3 * F), jnp.float32),
             pltpu.VMEM((LEN, 3 * F), jnp.bfloat16),
-            pltpu.VMEM((4, 4, ROWS, F), jnp.bfloat16),
+            pltpu.VMEM((LEN, F), jnp.bfloat16),
             pltpu.VMEM((KX, 4 * CW), jnp.bfloat16),
-            pltpu.VMEM((2, 4, ROWS, KX), jnp.bfloat16),
+            pltpu.VMEM((2, BQ, KX), jnp.bfloat16),
             pltpu.VMEM((CHUNKS, 4, ROWS, CW), jnp.bfloat16),
             pltpu.VMEM((CHUNKS, 3, ROWS, CW), jnp.bfloat16),
-            pltpu.VMEM((RC, LEN), jnp.float32),
             pltpu.VMEM((CHUNKS, ROWS, CW), jnp.bfloat16),
             dma((RINGS, SUBS)),
             dma((RINGS, SUBS, SPAN)),
@@ -518,9 +515,9 @@
             dma((2, 3)),
             dma((2, 3)),
             dma((CHUNKS,)),
+            dma((HEADS,)),
             dma((HEADS, 3)),
-            dma((HEADS, 3)),
-            dma((HEADS, 3)),
+            dma((HEADS,)),
             dma((HEADS, 3)),
             dma((CHUNKS,)),
             dma((CHUNKS,)),

time: 149 us -> 148 us (level)
  no operation moved by 1% of the time
where the time goes in v5:
time: 148 us
  Pallas kernels  146 us (99%)
    pallas_call x1, Pallas kernels, body(): pl.pallas_call(main_kernel, out_shape=(jax.ShapeDtypeStruct((ROWS, D), jn...  142 us
    pallas_call x1, Pallas kernels, body(): pl.pallas_call(finish_kernel, out_shape=(jax.ShapeDtypeStruct((ROWS, D),...  4.27 us

profile of v5, /device:TPU:0, one launch (start us, length us, event | category | flops | bytes accessed | tf_op | source)
XLA Modules:
  0.0 147.6 jit_solution(13600871420792187814)
XLA Ops:
  1.3 141.9 %sublayer.1 = (bf16[80,6144]{1,0:T(8,128)(2,1)}, bf16[1280,768]{1,0:T(8,128)(2,1)}, bf16[2,3,384,3072]{3,2,1,0:T(8,128)(2,1)}) custom-call(s32[1]{0:T(128)S(6)} %copy.12.len_ref, bf16[80,6144]{1,0:T(8,128)(2,1)} %tok_ref.1, f32[1,6144]{1,0:T(1,128)} %bitcast.8, f32[1,6144]{1,0:T(1,128)} %bitcast.9, bf16[3,6144,384]{2,1,0:T(8,128)(2,1)} %bitcast.6, ...), custom_call_target="tpu_custom_call" | custom-call | tf_op jit(solution)/shard_map/sublayer/pallas_call | solution.py:486
  143.2 4.3 %finish.1 = (bf16[80,6144]{1,0:T(8,128)(2,1)}, bf16[2,1536,384]{2,1,0:T(8,128)(2,1)}) custom-call(s32[1,10]{1,0:T(1,128)} %page_ref.1, s32[1]{0:T(128)S(6)} %copy.12.len_ref, bf16[80,6144]{1,0:T(8,128)(2,1)} %get-tuple-element.6.part_hbm, bf16[1280,768]{1,0:T(8,128)(2,1)} %get-tuple-element.7.new_hbm, bf16[2,1536,384]{2,1,0:T(8,128)(2,1)} %bitcast.7), custom_call_target="tpu_custom_call" | custom-call | tf_op jit(solution)/shard_map/finish/pallas_call | solution.py:540

commit v6 on v5

--- a/solution.py
+++ b/solution.py
@@ -30,8 +30,7 @@
 KX = 4 * F
 CHUNKS = 12
 LAG = 4
-QB = 128
-PIECES = ((0, 320, 0), (320, 640, 1), (640, 960, 2), (960, 1152, 3), (1152, 1280, 3))
+QB = 256
 SPAN = 4
 FORWARD_AT = 4
 SCALE2 = 1.4426950408889634 / (HD ** 0.5)
@@ -54,9 +53,10 @@
 
 
 def main_kernel(
-    len_ref, tok_ref, gain_ref, shift_ref, w_hbm, bq_ref, wo_hbm, bo_ref,
+    len_ref, tok_hbm, gain_hbm, shift_hbm, w_hbm, bq_hbm, wo_hbm, bo_hbm,
     out_ref, kv_hbm, g_hbm,
     ag, w, acc, qkv, att, wx, gat, psend, prec, out,
+    tok_ref, gain_ref, shift_ref, bq_ref, bo_ref, in_sem,
     ag_send, ag_recv, w_sem, kv_sem, out_sem,
     g_send, g1_recv, g2_recv, gy_recv, gf_recv, gd_recv,
     l_sem, az_send, az_recv, ax_send, ax_recv, p_send, p0_recv, p_recv,
@@ -85,6 +85,18 @@
     for peer in peers:
         pl.semaphore_signal(barrier, inc=1, device_id=peer, device_id_type=MESH)
 
+    inputs = [
+        pltpu.make_async_copy(src, dst, in_sem.at[i])
+        for i, (src, dst) in enumerate(
+            (
+                (tok_hbm, tok_ref), (gain_hbm, gain_ref), (shift_hbm, shift_ref),
+                (bq_hbm, bq_ref), (bo_hbm, bo_ref),
+            )
+        )
+    ]
+    for copy in inputs:
+        copy.start()
+
     w_copies = [
         pltpu.make_async_copy(w_hbm.at[c], w.at[:, pl.ds(c * F, F)], w_sem) for c in range(3)
     ]
@@ -130,6 +142,8 @@
                 ag[r, c, rows, :] = v[:, r * QW + c * CW : r * QW + (c + 1) * CW]
         return carry
 
+    for copy in inputs:
+        copy.wait()
     lax.fori_loop(0, ROWS // 16, norm_rows, 0)
 
     def slot(s):
@@ -293,18 +307,15 @@
 
     last = len_ref[0] - 1
 
-    def az_copy(h, lo, hi, qi, k):
-        src = att.at[pl.ds(lo, hi - lo), pl.ds(pl.multiple_of(h * HD, HD), HD)]
-        there = pl.ds(pl.multiple_of(k * F + h * HD, HD), HD)
-        return remote(
-            src, gat.at[1, pl.ds(lo - qi * BQ, hi - lo), there],
-            az_send.at[h], az_recv.at[h, k - 1], {"tp": qi * 4 + x},
-        )
+    def az_copy(h, j):
+        src = att.at[pl.ds(pl.multiple_of(lax.rem(z + j, 4) * BQ, 64), BQ), pl.ds(h * HD, HD)]
+        there = pl.ds((4 - j) * F + h * HD, HD)
+        return remote(src, gat.at[1, :, there], az_send.at[h], az_recv.at[h, 3 - j], along(1, j))
 
     def ax_copy(h, qi, j):
         block = pl.ds(pl.multiple_of((4 * qi + lax.rem(x + j, 4)) * ROWS, 16), ROWS)
-        src = att.at[block, pl.ds(pl.multiple_of(h * HD, HD), HD)]
-        there = pl.ds(pl.multiple_of((4 - j) * F + h * HD, HD), HD)
+        src = att.at[block, pl.ds(h * HD, HD)]
+        there = pl.ds((4 - j) * F + h * HD, HD)
         return remote(
             src, gat.at[0, pl.ds(qi * ROWS, ROWS), there], ax_send.at[h], ax_recv.at[h, 3 - j], along(0, j)
         )
@@ -318,47 +329,38 @@
         part = gat.at[axis, :, pl.ds(0, 3 * HD)]
         return remote(part, part, (ax_send, az_send)[axis].at[h], ax_recv.at[h, 0], along(0, 1))
 
-    def head(h, carry):
-        col = pl.multiple_of(h * HD, HD)
+    for h in range(HEADS):
+        q0, k0, v0 = h * HD, F + h * HD, 2 * F + h * HD
         for row in range(0, LEN, QB):
             kv = row + QB
             free = min(row, LEN // 2)
-            q = qkv[row : row + QB, pl.ds(col, HD)]
-            k = qkv[0:kv, pl.ds(F + col, HD)]
-            v = qkv[0:kv, pl.ds(2 * F + col, HD)]
-            sc = lax.dot_general(k, q, (((1,), (1,)), ((), ())), preferred_element_type=jnp.float32)
-            limit = jnp.minimum(lax.broadcasted_iota(jnp.int32, (1, QB), 1) + row, last)
-            key = lax.broadcasted_iota(jnp.int32, (kv - free, QB), 0) + free
-            masked = jnp.where(key <= limit, sc[free:], -1e30)
-            sc = jnp.concatenate([sc[:free], masked], axis=0) if free else masked
-            top = jnp.max(sc, axis=0, keepdims=True)
+            q = qkv[row:kv, q0 : q0 + HD]
+            k = qkv[0:kv, k0 : k0 + HD]
+            v = qkv[0:kv, v0 : v0 + HD]
+            sc = lax.dot_general(q, k, (((1,), (1,)), ((), ())), preferred_element_type=jnp.float32)
+            limit = jnp.minimum(lax.broadcasted_iota(jnp.int32, (QB, 1), 0) + row, last)
+            key = lax.broadcasted_iota(jnp.int32, (QB, kv - free), 1) + free
+            masked = jnp.where(key <= limit, sc[:, free:], -1e30)
+            sc = jnp.concatenate([sc[:, :free], masked], axis=1) if free else masked
+            top = jnp.max(sc, axis=-1, keepdims=True)
             e = jnp.exp2((sc - top) * SCALE2)
-            inv = 1.0 / jnp.sum(e, axis=0, keepdims=True)
+            inv = 1.0 / jnp.sum(e, axis=-1, keepdims=True)
             p = (e * inv).astype(jnp.bfloat16)
-            o = lax.dot_general(p, v, (((0,), (0,)), ((), ())), preferred_element_type=jnp.float32)
-            att[row : row + QB, pl.ds(col, HD)] = o.astype(jnp.bfloat16)
-            for lo, hi, qi in PIECES:
-                if row < hi <= kv:
-
-                    @pl.when(z != qi)
-                    def _():
-                        az_copy(h, lo, hi, qi, lax.rem(z - qi + 4, 4)).start()
-
-                    if hi == (qi + 1) * BQ:
-                        for j in (2, 1, 3):
-                            ax_copy(h, qi, j).start()
-
-        @pl.when(h == 0)
-        def _():
+            o = jnp.dot(p, v, preferred_element_type=jnp.float32)
+            att[row:kv, q0 : q0 + HD] = o.astype(jnp.bfloat16)
+            for qi in range(4):
+                if row < (qi + 1) * BQ <= kv:
+                    for j in (2, 1, 3):
+                        ax_copy(h, qi, j).start()
+        for j in (2, 1, 3):
+            az_copy(h, j).start()
+        if h == 0:
             for axis, k in blocks:
                 gd_copy(axis, k).wait_recv()
             for n in range(CHUNKS):
                 for k in range(4):
                     load(n, k).start()
 
-        return carry
-
-    lax.fori_loop(0, HEADS, head, 0)
     for b in range(4):
         gat[0, b * ROWS : (b + 1) * ROWS, 0:F] = att[pl.ds(pl.multiple_of((4 * b + x) * ROWS, 16), ROWS), :]
     gat[1, :, 0:F] = att[pl.ds(pl.multiple_of(z * BQ, 64), BQ), :]
@@ -479,7 +481,6 @@
 
 
 def body(tokens, ln_gain, ln_bias, w_qkv, b_qkv, w_out, b_out, kv_cache, page_table, lengths):
-    vmem = pl.BlockSpec(memory_space=pltpu.VMEM)
     anym = pl.BlockSpec(memory_space=pl.ANY)
     smem = pl.BlockSpec(memory_space=pltpu.SMEM)
     dma = pltpu.SemaphoreType.DMA
@@ -490,7 +491,7 @@
             jax.ShapeDtypeStruct((LEN, 2 * F), jnp.bfloat16),
             jax.ShapeDtypeStruct((2, 3, F, HC), jnp.bfloat16),
         ),
-        in_specs=[smem, vmem, vmem, vmem, anym, vmem, anym, vmem],
+        in_specs=[smem] + [anym] * 7,
         out_specs=(anym, anym, anym),
         scratch_shapes=[
             pltpu.VMEM((RINGS, SUBS, LEN, CW), jnp.bfloat16),
@@ -503,6 +504,12 @@
             pltpu.VMEM((CHUNKS, 4, ROWS, CW), jnp.bfloat16),
             pltpu.VMEM((CHUNKS, 3, ROWS, CW), jnp.bfloat16),
             pltpu.VMEM((CHUNKS, ROWS, CW), jnp.bfloat16),
+            pltpu.VMEM((ROWS, D), jnp.bfloat16),
+            pltpu.VMEM((1, D), jnp.float32),
+            pltpu.VMEM((1, D), jnp.float32),
+            pltpu.VMEM((3, F), jnp.float32),
+            pltpu.VMEM((1, D), jnp.float32),
+            dma((5,)),
             dma((RINGS, SUBS)),
             dma((RINGS, SUBS, SPAN)),
             dma,

time: 148 us -> 145 us (0.980)
  Pallas kernels: 146 us -> 143 us
    pallas_call x1, Pallas kernels: 142 us -> 139 us  [body(): pl.pallas_call(main_kernel, out_shape=(jax.ShapeDtypeStruct((ROWS, D), jn...]
where the time goes in v6:
time: 145 us
  Pallas kernels  143 us (99%)
  between operations  1.45 us (1%)
    pallas_call x1, Pallas kernels, body(): pl.pallas_call(main_kernel, out_shape=(jax.ShapeDtypeStruct((ROWS, D), jn...  139 us
    pallas_call x1, Pallas kernels, body(): pl.pallas_call(finish_kernel, out_shape=(jax.ShapeDtypeStruct((ROWS, D),...  4.27 us

profile of v6, /device:TPU:0, one launch (start us, length us, event | category | flops | bytes accessed | tf_op | source)
XLA Modules:
  0.0 144.8 jit_solution(6053966656212775621)
XLA Ops:
  1.3 139.0 %sublayer.1 = (bf16[80,6144]{1,0:T(8,128)(2,1)}, bf16[1280,768]{1,0:T(8,128)(2,1)}, bf16[2,3,384,3072]{3,2,1,0:T(8,128)(2,1)}) custom-call(s32[1]{0:T(128)S(6)} %copy.12.len_ref, bf16[80,6144]{1,0:T(8,128)(2,1)} %tok_hbm.1, f32[1,6144]{1,0:T(1,128)} %bitcast.8, f32[1,6144]{1,0:T(1,128)} %bitcast.9, bf16[3,6144,384]{2,1,0:T(8,128)(2,1)} %bitcast.6, ...), custom_call_target="tpu_custom_call" | custom-call | tf_op jit(solution)/shard_map/sublayer/pallas_call | solution.py:487
  140.3 4.3 %finish.1 = (bf16[80,6144]{1,0:T(8,128)(2,1)}, bf16[2,1536,384]{2,1,0:T(8,128)(2,1)}) custom-call(s32[1,10]{1,0:T(1,128)} %page_ref.1, s32[1]{0:T(128)S(6)} %copy.12.len_ref, bf16[80,6144]{1,0:T(8,128)(2,1)} %get-tuple-element.6.part_hbm, bf16[1280,768]{1,0:T(8,128)(2,1)} %get-tuple-element.7.new_hbm, bf16[2,1536,384]{2,1,0:T(8,128)(2,1)} %bitcast.7), custom_call_target="tpu_custom_call" | custom-call | tf_op jit(solution)/shard_map/finish/pallas_call | solution.py:547

commit v7 on v6

--- a/solution.py
+++ b/solution.py
@@ -31,6 +31,7 @@
 CHUNKS = 12
 LAG = 4
 QB = 256
+PIECES = ((0, 320, 0), (320, 640, 1), (640, 960, 2), (960, 1024, 3), (1024, 1280, 3))
 SPAN = 4
 FORWARD_AT = 4
 SCALE2 = 1.4426950408889634 / (HD ** 0.5)
@@ -307,10 +308,13 @@
 
     last = len_ref[0] - 1
 
-    def az_copy(h, j):
-        src = att.at[pl.ds(pl.multiple_of(lax.rem(z + j, 4) * BQ, 64), BQ), pl.ds(h * HD, HD)]
-        there = pl.ds((4 - j) * F + h * HD, HD)
-        return remote(src, gat.at[1, :, there], az_send.at[h], az_recv.at[h, 3 - j], along(1, j))
+    def az_copy(h, lo, hi, qi, k):
+        src = att.at[pl.ds(lo, hi - lo), pl.ds(h * HD, HD)]
+        there = pl.ds(pl.multiple_of(k * F + h * HD, HD), HD)
+        return remote(
+            src, gat.at[1, pl.ds(lo - qi * BQ, hi - lo), there],
+            az_send.at[h], az_recv.at[h, k - 1], {"tp": qi * 4 + x},
+        )
 
     def ax_copy(h, qi, j):
         block = pl.ds(pl.multiple_of((4 * qi + lax.rem(x + j, 4)) * ROWS, 16), ROWS)
@@ -348,12 +352,16 @@
             p = (e * inv).astype(jnp.bfloat16)
             o = jnp.dot(p, v, preferred_element_type=jnp.float32)
             att[row:kv, q0 : q0 + HD] = o.astype(jnp.bfloat16)
-            for qi in range(4):
-                if row < (qi + 1) * BQ <= kv:
-                    for j in (2, 1, 3):
-                        ax_copy(h, qi, j).start()
-        for j in (2, 1, 3):
-            az_copy(h, j).start()
+            for lo, hi, qi in PIECES:
+                if row < hi <= kv:
+
+                    @pl.when(z != qi)
+                    def _():
+                        az_copy(h, lo, hi, qi, lax.rem(z - qi + 4, 4)).start()
+
+                    if hi == (qi + 1) * BQ:
+                        for j in (2, 1, 3):
+                            ax_copy(h, qi, j).start()
         if h == 0:
             for axis, k in blocks:
                 gd_copy(axis, k).wait_recv()
@@ -438,46 +446,63 @@
 
 
 def finish_kernel(page_ref, len_ref, part_hbm, new_hbm, old_hbm, out_hbm, kv_hbm, part, new, kv, in_sem, out_sem):
-    group = SLOTS * PAGE // 4
-    news = [
-        pltpu.make_async_copy(new_hbm.at[pl.ds(g * BQ, BQ)], new.at[pl.ds(g * BQ, BQ)], in_sem.at[g])
-        for g in range(4)
-    ]
-    olds = [
-        pltpu.make_async_copy(
-            old_hbm.at[:, pl.ds(g * group, group)], kv.at[:, pl.ds(g * group, group)], in_sem.at[4 + g]
-        )
-        for g in range(4)
-    ]
-    kvs = [
-        pltpu.make_async_copy(
-            kv.at[:, pl.ds(g * group, group)], kv_hbm.at[:, pl.ds(g * group, group)], out_sem.at[g]
-        )
-        for g in range(4)
-    ]
-    load = pltpu.make_async_copy(part_hbm, part, in_sem.at[8])
-    store = pltpu.make_async_copy(part, out_hbm, out_sem.at[4])
-    for copy in [*news, *olds, load]:
-        copy.start()
-    for copy in news:
-        copy.wait()
-    for g in range(4):
-        olds[g].wait()
-        for i in range(g * SLOTS // 4, (g + 1) * SLOTS // 4):
-            page = jnp.int32(-1)
-            for p in range(PAGES):
-                page = jnp.where(page_ref[0, p] == i, p, page)
-            row = lax.broadcasted_iota(jnp.int32, (PAGE, 1), 0) + page * PAGE
-            written = (row < len_ref[0]) & (row >= 0)
-            rows = pl.ds(pl.multiple_of(jnp.maximum(page, 0) * PAGE, PAGE), PAGE)
+    load = pltpu.make_async_copy(part_hbm, part, in_sem.at[SLOTS])
+    load.start()
+
+    def rows_of(i):
+        return pl.ds(pl.multiple_of(i * PAGE, PAGE), PAGE)
+
+    def old_copy(i):
+        return pltpu.make_async_copy(old_hbm.at[:, rows_of(i)], kv.at[:, rows_of(i)], in_sem.at[i])
+
+    def kv_copy(i):
+        return pltpu.make_async_copy(kv.at[:, rows_of(i)], kv_hbm.at[:, rows_of(i)], out_sem.at[i])
+
+    def new_copy(page):
+        return pltpu.make_async_copy(new_hbm.at[rows_of(page)], new, in_sem.at[SLOTS + 1])
+
+    used = []
+    for i in range(SLOTS):
+        page = jnp.int32(-1)
+        for p in range(PAGES):
+            page = jnp.where(page_ref[0, p] == i, p, page)
+        count = jnp.where(page < 0, 0, jnp.clip(len_ref[0] - page * PAGE, 0, PAGE))
+        page = jnp.maximum(page, 0)
+        used.append((page, count))
+
+        @pl.when(count == PAGE)
+        def _():
             for c in range(2):
-                old = kv[c, i * PAGE : (i + 1) * PAGE, :]
-                kv[c, i * PAGE : (i + 1) * PAGE, :] = jnp.where(written, new[rows, c * F : (c + 1) * F], old)
-        kvs[g].start()
+                pltpu.make_async_copy(
+                    new_hbm.at[rows_of(page), pl.ds(c * F, F)], kv.at[c, rows_of(i)], in_sem.at[i]
+                ).start()
+
+        @pl.when(count < PAGE)
+        def _():
+            old_copy(i).start()
+
+        @pl.when((count > 0) & (count < PAGE))
+        def _():
+            new_copy(page).start()
+
+    store = pltpu.make_async_copy(part, out_hbm, out_sem.at[SLOTS])
     load.wait()
     store.start()
-    for copy in [*kvs, store]:
-        copy.wait()
+    for i, (page, count) in enumerate(used):
+        old_copy(i).wait()
+
+        @pl.when((count > 0) & (count < PAGE))
+        def _():
+            new_copy(page).wait()
+            written = lax.broadcasted_iota(jnp.int32, (PAGE, 1), 0) < count
+            for c in range(2):
+                rows = pl.ds(i * PAGE, PAGE)
+                kv[c, rows, :] = jnp.where(written, new[:, c * F : (c + 1) * F], kv[c, rows, :])
+
+        kv_copy(i).start()
+    for i in range(SLOTS):
+        kv_copy(i).wait()
+    store.wait()
 
 
 def body(tokens, ln_gain, ln_bias, w_qkv, b_qkv, w_out, b_out, kv_cache, page_table, lengths):
@@ -554,10 +579,10 @@
         out_specs=(anym, anym),
         scratch_shapes=[
             pltpu.VMEM((ROWS, D), jnp.bfloat16),
-            pltpu.VMEM((LEN, 2 * F), jnp.bfloat16),
+            pltpu.VMEM((PAGE, 2 * F), jnp.bfloat16),
             pltpu.VMEM((2, SLOTS * PAGE, F), jnp.bfloat16),
-            dma((9,)),
-            dma((5,)),
+            dma((SLOTS + 2,)),
+            dma((SLOTS + 1,)),
         ],
         name="finish",
     )(page_table, lengths, part, kv_new, kv_cache.reshape(2, SLOTS * PAGE, F))

time: 145 us -> 143 us (0.986)
  no operation moved by 1% of the time
where the time goes in v7:
time: 143 us
  Pallas kernels  142 us (99%)
  between operations  1.45 us (1%)
    pallas_call x1, Pallas kernels, body(): pl.pallas_call(main_kernel, out_shape=(jax.ShapeDtypeStruct((ROWS, D), jn...  138 us
    pallas_call x1, Pallas kernels, body(): pl.pallas_call(finish_kernel, out_shape=(jax.ShapeDtypeStruct((ROWS, D),...  3.82 us

profile of v7, /device:TPU:0, one launch (start us, length us, event | category | flops | bytes accessed | tf_op | source)
XLA Modules:
  0.0 143.3 jit_solution(4145381894336644182)
XLA Ops:
  1.3 138.1 %sublayer.1 = (bf16[80,6144]{1,0:T(8,128)(2,1)}, bf16[1280,768]{1,0:T(8,128)(2,1)}, bf16[2,3,384,3072]{3,2,1,0:T(8,128)(2,1)}) custom-call(s32[1]{0:T(128)S(6)} %copy.12.len_ref, bf16[80,6144]{1,0:T(8,128)(2,1)} %tok_hbm.1, f32[1,6144]{1,0:T(1,128)} %bitcast.8, f32[1,6144]{1,0:T(1,128)} %bitcast.9, bf16[3,6144,384]{2,1,0:T(8,128)(2,1)} %bitcast.6, ...), custom_call_target="tpu_custom_call" | custom-call | tf_op jit(solution)/shard_map/sublayer/pallas_call | solution.py:512
  139.4 3.8 %finish.1 = (bf16[80,6144]{1,0:T(8,128)(2,1)}, bf16[2,1536,384]{2,1,0:T(8,128)(2,1)}) custom-call(s32[1,10]{1,0:T(1,128)} %page_ref.1, s32[1]{0:T(128)S(6)} %copy.12.len_ref, bf16[80,6144]{1,0:T(8,128)(2,1)} %get-tuple-element.6.part_hbm, bf16[1280,768]{1,0:T(8,128)(2,1)} %get-tuple-element.7.new_hbm, bf16[2,1536,384]{2,1,0:T(8,128)(2,1)} %bitcast.7), custom_call_target="tpu_custom_call" | custom-call | tf_op jit(solution)/shard_map/finish/pallas_call | solution.py:572

commit v8 on v7

--- a/solution.py
+++ b/solution.py
@@ -362,7 +362,7 @@
                     if hi == (qi + 1) * BQ:
                         for j in (2, 1, 3):
                             ax_copy(h, qi, j).start()
-        if h == 0:
+        if h == 1:
             for axis, k in blocks:
                 gd_copy(axis, k).wait_recv()
             for n in range(CHUNKS):

time: 143 us -> 143 us (level)
  no operation moved by 1% of the time
where the time goes in v8:
time: 143 us
  Pallas kernels  142 us (99%)
  between operations  1.45 us (1%)
    pallas_call x1, Pallas kernels, body(): pl.pallas_call(main_kernel, out_shape=(jax.ShapeDtypeStruct((ROWS, D), jn...  138 us
    pallas_call x1, Pallas kernels, body(): pl.pallas_call(finish_kernel, out_shape=(jax.ShapeDtypeStruct((ROWS, D),...  3.82 us

profile of v8, /device:TPU:0, one launch (start us, length us, event | category | flops | bytes accessed | tf_op | source)
XLA Modules:
  0.0 143.3 jit_solution(9995292180877187674)
XLA Ops:
  1.3 138.1 %sublayer.1 = (bf16[80,6144]{1,0:T(8,128)(2,1)}, bf16[1280,768]{1,0:T(8,128)(2,1)}, bf16[2,3,384,3072]{3,2,1,0:T(8,128)(2,1)}) custom-call(s32[1]{0:T(128)S(6)} %copy.12.len_ref, bf16[80,6144]{1,0:T(8,128)(2,1)} %tok_hbm.1, f32[1,6144]{1,0:T(1,128)} %bitcast.8, f32[1,6144]{1,0:T(1,128)} %bitcast.9, bf16[3,6144,384]{2,1,0:T(8,128)(2,1)} %bitcast.6, ...), custom_call_target="tpu_custom_call" | custom-call | tf_op jit(solution)/shard_map/sublayer/pallas_call | solution.py:512
  139.4 3.8 %finish.1 = (bf16[80,6144]{1,0:T(8,128)(2,1)}, bf16[2,1536,384]{2,1,0:T(8,128)(2,1)}) custom-call(s32[1,10]{1,0:T(1,128)} %page_ref.1, s32[1]{0:T(128)S(6)} %copy.12.len_ref, bf16[80,6144]{1,0:T(8,128)(2,1)} %get-tuple-element.6.part_hbm, bf16[1280,768]{1,0:T(8,128)(2,1)} %get-tuple-element.7.new_hbm, bf16[2,1536,384]{2,1,0:T(8,128)(2,1)} %bitcast.7), custom_call_target="tpu_custom_call" | custom-call | tf_op jit(solution)/shard_map/finish/pallas_call | solution.py:572
